TPU v7x, 32 devices: a whole 2x2x4 slice. The times are simulated.
32 devices in a mesh: px: 8 (over z, y), py: 4 (over x, core).
Axes of the slice: x: 2, y: 2, z: 4, core: 2. Of those that a mesh axis runs over, the one named last changes fastest.
Arguments:
- initial_field: float32 [1, 2048, 2048], P(None, ('px', 'py')), may hold values from -6 to 6
- target_field: float32 [1, 2048, 2048], P(None, ('px', 'py')), may hold values from -6 to 6
- forcing: float32 [2, 2048, 2048], P(None, ('px', 'py')), may hold values from -6 to 6
Outputs:
- next_field: float32 [1, 2048, 2048], P(None, ('px', 'py'))
- objective: float32 [], replicated
- field_grad: float32 [1, 2048, 2048], P(None, ('px', 'py'))
- forcing_grad: float32 [2, 2048, 2048], P(None, ('px', 'py'))
All inputs are finite; a program needn't handle non-finite values.
Results may differ from a plain program's by a relative error of at most 0.00014.
Values sent between devices are 32-bit elements; how exact they have to be, the bound alone decides.
No kernel may reach another device: no remote copies, remote signals or barrier semaphores. Data moves between devices by JAX's collectives and lax.ppermute only.
A program may use at most 128 MiB of HBM per device.

v0:
```python
import math

import jax
import jax.numpy as jnp
from jax import lax
from jax.sharding import PartitionSpec as P

time_step = 0.25
highest = lax.Precision.HIGHEST


def factor_pair(length):
    first_len = int(math.isqrt(length))
    while length % first_len:
        first_len -= 1
    return (first_len, length // first_len)


def phases(row_count, col_count, period, sign_value, factor):
    product = (
        jnp.arange(row_count, dtype=jnp.int32)[:, None]
        * jnp.arange(col_count, dtype=jnp.int32)[None, :]
        % period
    )
    angles = product.astype(jnp.float32) * (2.0 * math.pi / period)
    return (factor * jnp.cos(angles), sign_value * factor * jnp.sin(angles))


def complex_einsum(formula, left_real, left_imag, table_pair):
    real_term = jnp.einsum(formula, left_real, table_pair[0], precision=highest)
    imag_term = jnp.einsum(formula, left_real, table_pair[1], precision=highest)
    if left_imag is None:
        return (real_term, imag_term)
    real_term = real_term - jnp.einsum(formula, left_imag, table_pair[1], precision=highest)
    imag_term = imag_term + jnp.einsum(formula, left_imag, table_pair[0], precision=highest)
    return (real_term, imag_term)


def transform(real_part, imag_part, sign_value, leading, real_only):
    if leading:
        members, length, span_rows = real_part.shape
        first_len, second_len = factor_pair(length)
        new_shape = (members, first_len, second_len, span_rows)
        formula = "mabr,ak->mrkb"
    else:
        members, span_rows, length = real_part.shape
        first_len, second_len = factor_pair(length)
        new_shape = (members, span_rows, first_len, second_len)
        formula = "mrab,ak->mrkb"
    shaped_real = real_part.reshape(new_shape)
    shaped_imag = None if imag_part is None else imag_part.reshape(new_shape)
    sectioned_out = complex_einsum(
        formula, shaped_real, shaped_imag, phases(first_len, first_len, first_len, sign_value, 1.0)
    )
    twiddle = phases(first_len, second_len, length, sign_value, 1.0 / math.sqrt(length))
    turned_real = sectioned_out[0] * twiddle[0] - sectioned_out[1] * twiddle[1]
    turned_imag = sectioned_out[0] * twiddle[1] + sectioned_out[1] * twiddle[0]
    last_table = phases(second_len, second_len, second_len, sign_value, 1.0)
    final_formula = "mrkb,bq->mrqk"
    if real_only:
        out_real = jnp.einsum(final_formula, turned_real, last_table[0], precision=highest)
        out_real = out_real - jnp.einsum(
            final_formula, turned_imag, last_table[1], precision=highest
        )
        return (out_real.reshape(members, span_rows, length), None)
    out_real, out_imag = complex_einsum(final_formula, turned_real, turned_imag, last_table)
    return (
        out_real.reshape(members, span_rows, length),
        out_imag.reshape(members, span_rows, length),
    )


def regroup(real_part, imag_part):
    moved_real, moved_imag = (
        lax.all_to_all(real_part, ("px", "py"), split_axis=2, concat_axis=1, tiled=True),
        lax.all_to_all(imag_part, ("px", "py"), split_axis=2, concat_axis=1, tiled=True),
    )
    return (moved_real, moved_imag)


def spectral(real_part, imag_part):
    first_pass = transform(real_part, imag_part, -1.0, False, False)
    moved = regroup(first_pass[0], first_pass[1])
    return transform(moved[0], moved[1], -1.0, True, False)


def physical(real_part, imag_part, real_only):
    first_pass = transform(real_part, imag_part, 1.0, False, False)
    moved = regroup(first_pass[0], first_pass[1])
    return transform(moved[0], moved[1], 1.0, True, real_only)


def waves_of(position, count):
    signed = jnp.where(position < count // 2, position, position - count)
    waves = 4.0 * signed.astype(jnp.float32) / count
    derive = jnp.where(position == count // 2, jnp.float32(0.0), waves)
    return (waves, derive)


def per_device(initial_field, target_field, forcing):
    members = initial_field.shape[0]
    full_second = initial_field.shape[2]
    spec_rows = forcing.shape[1]
    full_first = forcing.shape[2]
    device = lax.axis_index(("px", "py"))
    position_first = jnp.arange(full_first, dtype=jnp.int32)
    position_second = device * spec_rows + jnp.arange(spec_rows, dtype=jnp.int32)
    wave_first, deriv_first = waves_of(position_first, full_first)
    wave_second, deriv_second = waves_of(position_second, full_second)
    wave_first = wave_first[None, :]
    deriv_first = deriv_first[None, :]
    wave_second = wave_second[:, None]
    deriv_second = deriv_second[:, None]
    wave_square = wave_first * wave_first + wave_second * wave_second
    denominator = 1.0 + time_step * (wave_square * wave_square - wave_square)
    state_real, state_imag = spectral(initial_field, None)
    slope_real = -deriv_first * state_imag - deriv_second * state_real
    slope_imag = deriv_first * state_real - deriv_second * state_imag
    grad_first, grad_second = physical(slope_real, slope_imag, False)
    nonlinear = -0.5 * (grad_first * grad_first + grad_second * grad_second)
    nonlinear_real, nonlinear_imag = spectral(nonlinear, None)
    next_real = (state_real + time_step * (nonlinear_real + forcing[0])) / denominator
    next_imag = (state_imag + time_step * (nonlinear_imag + forcing[1])) / denominator
    next_field, unused_part = physical(next_real, next_imag, True)
    residual = next_field - target_field
    total = lax.psum(0.5 * jnp.sum(residual * residual), ("px", "py"))
    objective = total / (members * full_first * full_second)
    misfit_real, misfit_imag = spectral(residual, None)
    coef_real = misfit_real / denominator
    coef_imag = misfit_imag / denominator
    forcing_grad = time_step * jnp.stack([jnp.sum(coef_real, axis=0), jnp.sum(coef_imag, axis=0)])
    multiplier, unused_other = physical(time_step * coef_real, time_step * coef_imag, True)
    joint_real, joint_imag = spectral(multiplier * grad_first, multiplier * grad_second)
    total_real = coef_real - deriv_first * joint_imag + deriv_second * joint_real
    total_imag = coef_imag + deriv_first * joint_real + deriv_second * joint_imag
    field_grad, unused_last = physical(total_real, total_imag, True)
    return (next_field, objective, field_grad, forcing_grad)


def solution(mesh):
    return jax.shard_map(
        per_device,
        mesh=mesh,
        in_specs=(
            P(None, ("px", "py"), None),
            P(None, ("px", "py"), None),
            P(None, ("px", "py"), None),
        ),
        out_specs=(
            P(None, ("px", "py"), None),
            P(),
            P(None, ("px", "py"), None),
            P(None, ("px", "py"), None),
        ),
        check_vma=False,
    )
```

profile of v0, /device:TPU:0, one launch (start us, length us, event | category | flops | bytes accessed | tf_op | source)
XLA Modules:
  0.0 883.1 jit_solution(13582286991271843873)
XLA Ops:
  13.7 10.5 %reduce = f32[2048,64]{1,0:T(8,128)S(1)} reduce(f32[2048,1,64]{2,1,0:T(1,128)} %bitcast.931, f32[]{:T(128)} %broadcast.1623), dimensions={1}, to_apply=%bitcast.761.reduce_sub_computation | reduce | bytes 1048580
  25.6 7.3 all-to-all-start
  40.6 9.3 %reduce.2 = f32[2048,64]{1,0:T(8,128)S(1)} reduce(f32[2048,1,64]{2,1,0:T(1,128)S(1)} %bitcast.932, f32[]{:T(128)} %broadcast.1623), dimensions={1}, to_apply=%bitcast.763.reduce_sub_computation | reduce | bytes 1048580
  65.1 8.1 all-to-all-done.1
  123.8 11.5 %reduce.4 = f32[2048,64]{1,0:T(8,128)} reduce(f32[2048,1,64]{2,1,0:T(1,128)} %bitcast.933, f32[]{:T(128)} %broadcast.1623), dimensions={1}, to_apply=%bitcast.765.reduce_sub_computation | reduce | bytes 1048580
  151.2 10.3 %reduce.6 = f32[2048,64]{1,0:T(8,128)S(1)} reduce(f32[2048,1,64]{2,1,0:T(1,128)} %bitcast.934, f32[]{:T(128)} %broadcast.1623), dimensions={1}, to_apply=%bitcast.767.reduce_sub_computation | reduce | bytes 1048580
  162.9 6.3 all-to-all-start.3
  234.5 11.3 %reduce.8 = f32[2048,64]{1,0:T(8,128)} reduce(f32[2048,1,64]{2,1,0:T(1,128)} %bitcast.935, f32[]{:T(128)} %broadcast.1623), dimensions={1}, to_apply=%bitcast.769.reduce_sub_computation | reduce | bytes 1048580
  262.0 10.3 %reduce.10 = f32[2048,64]{1,0:T(8,128)S(1)} reduce(f32[2048,1,64]{2,1,0:T(1,128)} %bitcast.936, f32[]{:T(128)} %broadcast.1623), dimensions={1}, to_apply=%bitcast.771.reduce_sub_computation | reduce | bytes 1048580
  349.9 10.3 %reduce.12 = f32[2048,64]{1,0:T(8,128)S(1)} reduce(f32[2048,1,64]{2,1,0:T(1,128)} %bitcast.937, f32[]{:T(128)} %broadcast.1623), dimensions={1}, to_apply=%bitcast.773.reduce_sub_computation | reduce | bytes 1048580
  375.6 9.3 %reduce.14 = f32[2048,64]{1,0:T(8,128)S(1)} reduce(f32[2048,1,64]{2,1,0:T(1,128)S(1)} %bitcast.938, f32[]{:T(128)} %broadcast.1623), dimensions={1}, to_apply=%bitcast.775.reduce_sub_computation | reduce | bytes 1048580
  401.2 6.8 all-to-all-done.7
  436.4 10.3 %reduce.16 = f32[2048,64]{1,0:T(8,128)S(1)} reduce(f32[2048,1,64]{2,1,0:T(1,128)} %bitcast.939, f32[]{:T(128)} %broadcast.1623), dimensions={1}, to_apply=%bitcast.777.reduce_sub_computation | reduce | bytes 1048580
  458.7 9.3 %reduce.18 = f32[2048,64]{1,0:T(8,128)S(1)} reduce(f32[2048,1,64]{2,1,0:T(1,128)S(1)} %bitcast.940, f32[]{:T(128)} %broadcast.1623), dimensions={1}, to_apply=%bitcast.779.reduce_sub_computation | reduce | bytes 1048580
  483.0 8.3 all-to-all-done.9
  542.0 11.3 %reduce.20 = f32[2048,64]{1,0:T(8,128)} reduce(f32[2048,1,64]{2,1,0:T(1,128)} %bitcast.941, f32[]{:T(128)} %broadcast.1623), dimensions={1}, to_apply=%bitcast.781.reduce_sub_computation | reduce | bytes 1048580
  569.3 10.3 %reduce.22 = f32[2048,64]{1,0:T(8,128)S(1)} reduce(f32[2048,1,64]{2,1,0:T(1,128)} %bitcast.942, f32[]{:T(128)} %broadcast.1623), dimensions={1}, to_apply=%bitcast.783.reduce_sub_computation | reduce | bytes 1048580
  581.0 6.3 all-to-all-start.11
  645.4 11.3 %reduce.24 = f32[2048,64]{1,0:T(8,128)} reduce(f32[2048,1,64]{2,1,0:T(1,128)} %bitcast.943, f32[]{:T(128)} %broadcast.1623), dimensions={1}, to_apply=%bitcast.785.reduce_sub_computation | reduce | bytes 1048580
  672.8 10.3 %reduce.26 = f32[2048,64]{1,0:T(8,128)S(1)} reduce(f32[2048,1,64]{2,1,0:T(1,128)} %bitcast.944, f32[]{:T(128)} %broadcast.1623), dimensions={1}, to_apply=%bitcast.787.reduce_sub_computation | reduce | bytes 1048580
  684.5 6.5 all-to-all-start.13
  765.7 11.5 %reduce.28 = f32[2048,64]{1,0:T(8,128)} reduce(f32[2048,1,64]{2,1,0:T(1,128)} %bitcast.945, f32[]{:T(128)} %broadcast.1623), dimensions={1}, to_apply=%bitcast.789.reduce_sub_computation | reduce | bytes 1048580
  783.8 40.5 %psum.7 = f32[]{:T(128)} all-reduce(f32[]{:T(128)S(6)} %mul_shard_map.3), channel_id=1, replica_groups=mesh['px'=8,'py'=4] {'px','py'}, use_global_device_ids=true, to_apply=%region_1.2 | all-reduce | flops 1 | bytes 8 | tf_op jit(solution)/shard_map/psum | solution.py:126
  837.1 10.3 %reduce.30 = f32[2048,64]{1,0:T(8,128)S(1)} reduce(f32[2048,1,64]{2,1,0:T(1,128)} %bitcast.946, f32[]{:T(128)} %broadcast.1623), dimensions={1}, to_apply=%bitcast.791.reduce_sub_computation | reduce | bytes 1048580
  (358 shorter events, 620.8 us)
Async XLA Ops:
  25.6 25.7 %all-to-all-start = ((f32[32,1,4096]{2,1,0:T(1,128)}), f32[32,1,4096]{2,1,0:T(1,128)S(1)}, u32[]{:S(2)}, u32[]{:S(2)}) async-start(f32[32,1,4096]{2,1,0:T(1,128)} %reshape.1269), calls=%async_computation | async-start | bytes 1048576 | tf_op jit(solution)/shard_map/all_to_all | solution.py:75
  51.3 21.9 %all-to-all-start.1 = ((f32[32,1,4096]{2,1,0:T(1,128)}), f32[32,1,4096]{2,1,0:T(1,128)S(1)}, u32[]{:S(2)}, u32[]{:S(2)}) async-start(f32[32,1,4096]{2,1,0:T(1,128)} %reshape.1271), calls=%async_computation.1 | async-start | bytes 1048576 | tf_op jit(solution)/shard_map/all_to_all | solution.py:76
  115.2 7.1 copy-start.10
  138.0 24.9 %all-to-all-start.2 = ((f32[32,1,4096]{2,1,0:T(1,128)}), f32[32,1,4096]{2,1,0:T(1,128)}, u32[]{:S(2)}, u32[]{:S(2)}) async-start(f32[32,1,4096]{2,1,0:T(1,128)} %reshape.1273), calls=%async_computation.2 | async-start | bytes 1048576 | tf_op jit(solution)/shard_map/all_to_all | solution.py:75
  162.9 21.9 %all-to-all-start.3 = ((f32[32,1,4096]{2,1,0:T(1,128)}), f32[32,1,4096]{2,1,0:T(1,128)}, u32[]{:S(2)}, u32[]{:S(2)}) async-start(f32[32,1,4096]{2,1,0:T(1,128)} %reshape.1275), calls=%async_computation.3 | async-start | bytes 1048576 | tf_op jit(solution)/shard_map/all_to_all | solution.py:76
  225.7 7.2 copy-start.13
  248.5 25.3 %all-to-all-start.4 = ((f32[32,1,4096]{2,1,0:T(1,128)}), f32[32,1,4096]{2,1,0:T(1,128)}, u32[]{:S(2)}, u32[]{:S(2)}) async-start(f32[32,1,4096]{2,1,0:T(1,128)} %reshape.1277), calls=%async_computation.4 | async-start | bytes 1048576 | tf_op jit(solution)/shard_map/all_to_all | solution.py:75
  273.8 21.8 %all-to-all-start.5 = ((f32[32,1,4096]{2,1,0:T(1,128)}), f32[32,1,4096]{2,1,0:T(1,128)}, u32[]{:S(2)}, u32[]{:S(2)}) async-start(f32[32,1,4096]{2,1,0:T(1,128)} %reshape.1279), calls=%async_computation.5 | async-start | bytes 1048576 | tf_op jit(solution)/shard_map/all_to_all | solution.py:76
  320.5 5.1 copy-start.20
  361.6 24.7 %all-to-all-start.6 = ((f32[32,1,4096]{2,1,0:T(1,128)}), f32[32,1,4096]{2,1,0:T(1,128)}, u32[]{:S(2)}, u32[]{:S(2)}) async-start(f32[32,1,4096]{2,1,0:T(1,128)} %reshape.1281), calls=%async_computation.6 | async-start | bytes 1048576 | tf_op jit(solution)/shard_map/all_to_all | solution.py:75
  384.8 7.7 copy-start.37
  386.3 21.7 %all-to-all-start.7 = ((f32[32,1,4096]{2,1,0:T(1,128)}), f32[32,1,4096]{2,1,0:T(1,128)}, u32[]{:S(2)}, u32[]{:S(2)}) async-start(f32[32,1,4096]{2,1,0:T(1,128)} %reshape.1283), calls=%async_computation.7 | async-start | bytes 1048576 | tf_op jit(solution)/shard_map/all_to_all | solution.py:76
  448.1 21.3 %all-to-all-start.8 = ((f32[32,1,4096]{2,1,0:T(1,128)}), f32[32,1,4096]{2,1,0:T(1,128)S(1)}, u32[]{:S(2)}, u32[]{:S(2)}) async-start(f32[32,1,4096]{2,1,0:T(1,128)} %reshape.1285), calls=%async_computation.8 | async-start | bytes 1048576 | tf_op jit(solution)/shard_map/all_to_all | solution.py:75
  469.4 21.9 %all-to-all-start.9 = ((f32[32,1,4096]{2,1,0:T(1,128)}), f32[32,1,4096]{2,1,0:T(1,128)S(1)}, u32[]{:S(2)}, u32[]{:S(2)}) async-start(f32[32,1,4096]{2,1,0:T(1,128)} %reshape.1287), calls=%async_computation.9 | async-start | bytes 1048576 | tf_op jit(solution)/shard_map/all_to_all | solution.py:76
  533.3 7.0 copy-start.11
  555.9 25.1 %all-to-all-start.10 = ((f32[32,1,4096]{2,1,0:T(1,128)}), f32[32,1,4096]{2,1,0:T(1,128)}, u32[]{:S(2)}, u32[]{:S(2)}) async-start(f32[32,1,4096]{2,1,0:T(1,128)} %reshape.1289), calls=%async_computation.10 | async-start | bytes 1048576 | tf_op jit(solution)/shard_map/all_to_all | solution.py:75
  581.0 21.7 %all-to-all-start.11 = ((f32[32,1,4096]{2,1,0:T(1,128)}), f32[32,1,4096]{2,1,0:T(1,128)}, u32[]{:S(2)}, u32[]{:S(2)}) async-start(f32[32,1,4096]{2,1,0:T(1,128)} %reshape.1291), calls=%async_computation.11 | async-start | bytes 1048576 | tf_op jit(solution)/shard_map/all_to_all | solution.py:76
  636.6 7.2 copy-start.9
  659.4 25.1 %all-to-all-start.12 = ((f32[32,1,4096]{2,1,0:T(1,128)}), f32[32,1,4096]{2,1,0:T(1,128)}, u32[]{:S(2)}, u32[]{:S(2)}) async-start(f32[32,1,4096]{2,1,0:T(1,128)} %reshape.1293), calls=%async_computation.12 | async-start | bytes 1048576 | tf_op jit(solution)/shard_map/all_to_all | solution.py:75
  684.5 22.1 %all-to-all-start.13 = ((f32[32,1,4096]{2,1,0:T(1,128)}), f32[32,1,4096]{2,1,0:T(1,128)}, u32[]{:S(2)}, u32[]{:S(2)}) async-start(f32[32,1,4096]{2,1,0:T(1,128)} %reshape.1295), calls=%async_computation.13 | async-start | bytes 1048576 | tf_op jit(solution)/shard_map/all_to_all | solution.py:76
  731.2 5.1 copy-start.23
  757.0 7.0 copy-start.8
  779.8 69.1 %all-to-all-start.14 = ((f32[32,1,4096]{2,1,0:T(1,128)}), f32[32,1,4096]{2,1,0:T(1,128)}, u32[]{:S(2)}, u32[]{:S(2)}) async-start(f32[32,1,4096]{2,1,0:T(1,128)} %reshape.1297), calls=%async_computation.14 | async-start | bytes 1048576 | tf_op jit(solution)/shard_map/all_to_all | solution.py:75
  848.9 20.5 %all-to-all-start.15 = ((f32[32,1,4096]{2,1,0:T(1,128)}), f32[32,1,4096]{2,1,0:T(1,128)S(1)}, u32[]{:S(2)}, u32[]{:S(2)}) async-start(f32[32,1,4096]{2,1,0:T(1,128)} %reshape.1299), calls=%async_computation.15 | async-start | bytes 1048576 | tf_op jit(solution)/shard_map/all_to_all | solution.py:76
  (30 other events, 62.3 us)
where the time goes:
time: 894 us; the launch traced here: 883 us
  matrix products  321 us (36%)
  other arithmetic  217 us (24%)
  local copies, waits for them, and re-layouts  176 us (20%)
  starting transfers between devices  83.1 us (9%)
  blocking collectives  40.5 us (5%)
  waiting for transfers between devices  40.4 us (5%)
    unnamed x16, other arithmetic  167 us
    dot_general x29, matrix products, complex_einsum(): imag_term = jnp.einsum(formula, left_real, table_pair[1], precision=highest)  81.2 us
    dot_general x29, matrix products, complex_einsum(): real_term = jnp.einsum(formula, left_real, table_pair[0], precision=highest)  80 us
    unnamed x115, local copies, waits for them, and re-layouts  74.6 us
    dot_general x26, matrix products, complex_einsum(): jnp.einsum(formula, left_imag, table_pair[1], precision=highest)  74.2 us
    dot_general x26, matrix products, complex_einsum(): jnp.einsum(formula, left_imag, table_pair[0], precision=highest)  73.5 us
    all_to_all x8, starting transfers between devices, regroup(): lax.all_to_all(imag_part, ('px', 'py'), split_axis=2, concat_axis=1, tile...  49.1 us
    psum x1, blocking collectives, per_device(): total = lax.psum(0.5 * jnp.sum(residual * residual), ('px', 'py'))  40.5 us
  transfers between devices with their start and end apart: 16, of which 8 were waited for; matrix products, arithmetic and copies ran while one was open for 28% of the time, Pallas kernels for 0%

commit v1 on v0

--- a/solution.py
+++ b/solution.py
@@ -2,7 +2,10 @@
 
 import jax
 import jax.numpy as jnp
+import numpy as np
 from jax import lax
+from jax.experimental import pallas as pl
+from jax.experimental.pallas import tpu as pltpu
 from jax.sharding import PartitionSpec as P
 
 time_step = 0.25
@@ -97,7 +100,7 @@
     return (waves, derive)
 
 
-def per_device(initial_field, target_field, forcing):
+def per_device_plain(initial_field, target_field, forcing):
     members = initial_field.shape[0]
     full_second = initial_field.shape[2]
     spec_rows = forcing.shape[1]
@@ -137,6 +140,834 @@
     return (next_field, objective, field_grad, forcing_grad)
 
 
+def split_of(value):
+    high = value.astype(jnp.bfloat16)
+    low = (value - high.astype(jnp.float32)).astype(jnp.bfloat16)
+    return high, low
+
+
+def dots(high, low, table_high, table_low):
+    def one(left, right):
+        return jnp.dot(left, right, preferred_element_type=jnp.float32)
+
+    return one(high, table_high) + (one(low, table_high) + one(high, table_low))
+
+
+def turn(pair, cosine, sine):
+    real, imag = pair
+    return real * cosine - imag * sine, imag * cosine + real * sine
+
+
+def butterflies(values, sign):
+    count = len(values)
+    if count == 1:
+        return values
+    even = butterflies(values[0::2], sign)
+    odd = butterflies(values[1::2], sign)
+    half = count // 2
+    first, second = [], []
+    root = math.sqrt(0.5)
+    for place in range(half):
+        real, imag = odd[place]
+        if place == 0:
+            turned = (real, imag)
+        elif 4 * place == count:
+            turned = (-sign * imag, sign * real)
+        elif 8 * place == count:
+            turned = (root * (real - sign * imag), root * (imag + sign * real))
+        elif 8 * place == 3 * count:
+            turned = (root * (-real - sign * imag), root * (sign * real - imag))
+        else:
+            angle = 2.0 * math.pi * place / count
+            turned = turn((real, imag), math.cos(angle), sign * math.sin(angle))
+        base_real, base_imag = even[place]
+        first.append((base_real + turned[0], base_imag + turned[1]))
+        second.append((base_real - turned[0], base_imag - turned[1]))
+    return first + second
+
+
+def np_split(table):
+    high = np.asarray(table, np.float32).astype(jnp.bfloat16)
+    low = (np.asarray(table, np.float64) - high.astype(np.float64)).astype(jnp.bfloat16)
+    return jnp.asarray(high), jnp.asarray(low)
+
+
+class Tables:
+    def __init__(self, length, parts):
+        radix = 8
+        inner = length // radix
+        lanes = length // parts
+        scale = 1.0 / math.sqrt(length)
+        spot = np.arange(inner)
+        angle = 2.0 * np.pi * (np.outer(spot, spot) % inner) / inner
+        self.row_pair = np_split(scale * np.concatenate([np.cos(angle), np.sin(angle)], 1))
+        classes = np.arange(radix)
+        angle = 2.0 * np.pi * np.outer(classes, spot) / length
+        self.row_turn = (
+            jnp.asarray(np.cos(angle), jnp.float32),
+            jnp.asarray(np.sin(angle), jnp.float32),
+        )
+        half = inner // 2
+        front = np.arange(half)
+        angle = 2.0 * np.pi * (np.outer(front, spot) % inner) / inner
+        real_rows, imag_rows = 2.0 * np.cos(angle), -2.0 * np.sin(angle)
+        real_rows[0] = 1.0
+        imag_rows[0] = np.where(spot % 2 == 0, 1.0, -1.0)
+        self.even_pair = np_split(scale * np.concatenate([real_rows, imag_rows], 0))
+        angle = 2.0 * np.pi * (np.outer(4 + radix * (front + half), spot) % length) / length
+        self.odd_pair = np_split(
+            scale * np.concatenate([2.0 * np.cos(angle), -2.0 * np.sin(angle)], 0)
+        )
+        place = np.arange(lanes)
+        angle = 2.0 * np.pi * (np.outer(place, place) % lanes) / lanes
+        eye = np.eye(inner // lanes)
+        self.col_pair = np_split(
+            scale * np.concatenate([np.kron(eye, np.cos(angle)), np.kron(eye, np.sin(angle))], 1)
+        )
+        outer = np.arange(parts)
+        angle = 2.0 * np.pi * np.outer(outer, np.tile(place, inner // lanes)) / length
+        self.col_turn = (
+            jnp.asarray(np.cos(angle), jnp.float32),
+            jnp.asarray(np.sin(angle), jnp.float32),
+        )
+        index = outer[:, None] + parts * np.tile(place, inner // lanes)[None, :]
+        signed = np.where(index < length // 2, index, index - length)
+        waves = 4.0 * signed / length
+        self.col_wave = waves
+        self.col_deriv = jnp.asarray(np.where(index == length // 2, 0.0, waves), jnp.float32)
+        index = np.stack([radix * spot + one for one in range(4)])
+        index[0, half:] += 4
+        signed = np.where(index < length // 2, index, index - length)
+        waves = 4.0 * signed / length
+        waves[0, 0] = 0.0
+        self.row_deriv = jnp.asarray(waves, jnp.float32)
+
+
+def eight_real(blocks):
+    plus = [blocks[i] + blocks[i + 4] for i in range(4)]
+    minus = [blocks[i] - blocks[i + 4] for i in range(4)]
+    root = math.sqrt(0.5)
+    even, odd = plus[0] + plus[2], plus[1] + plus[3]
+    near, far = root * (minus[1] - minus[3]), root * (minus[1] + minus[3])
+    return {
+        0: even + odd,
+        4: even - odd,
+        1: (minus[0] + near, -minus[2] - far),
+        2: (plus[0] - plus[2], plus[3] - plus[1]),
+        3: (minus[0] - near, minus[2] - far),
+    }
+
+
+def rows_forward(load, high, low, product, pair, spin, other):
+    for row in range(0, 64, 16):
+        for lane in range(0, 256, 128):
+            rows, lanes = slice(row, row + 16), slice(lane, lane + 128)
+            mixed = eight_real([load(one, rows, lanes) for one in range(8)])
+
+            def spun(kind, real, imag):
+                cosine = spin[0][kind : kind + 1, lanes]
+                sine = spin[1][kind : kind + 1, lanes]
+                if imag is None:
+                    return real * cosine, -real * sine
+                return real * cosine + imag * sine, imag * cosine - real * sine
+
+            out = [None] * 9
+            out[0] = mixed[0]
+            for one in (1, 2, 3):
+                if other:
+                    real, imag = mixed[4 - one]
+                    out[one], out[3 + one] = spun(4 + one, real, -imag)
+                else:
+                    out[one], out[3 + one] = spun(one, *mixed[one])
+            out[7], out[8] = spun(4, mixed[4], None)
+            for place in range(9):
+                top, bottom = split_of(out[place])
+                at = slice(64 * place + row, 64 * place + row + 16)
+                high[at, lanes] = top
+                low[at, lanes] = bottom
+    product[0:576, :] = dots(high[0:576, :], low[0:576, :], pair[0][...], pair[1][...])
+
+    def cosine(place, lanes=slice(0, 256)):
+        return product[64 * place : 64 * place + 64, lanes]
+
+    def sine(place, lanes=slice(0, 256)):
+        moved = slice(lanes.start + 256, lanes.stop + 256)
+        return product[64 * place : 64 * place + 64, moved]
+
+    front, back = slice(0, 128), slice(128, 256)
+    if other:
+        real = [jnp.concatenate([cosine(7, front) + sine(8, front), cosine(0, back)], 1)]
+        imag = [jnp.concatenate([cosine(8, front) - sine(7, front), -sine(0, back)], 1)]
+    else:
+        lane = lax.broadcasted_iota(jnp.int32, (64, 128), 1)
+        first = jnp.where(lane == 0, cosine(0, back), -sine(0, front))
+        real = [jnp.concatenate([cosine(0, front), cosine(7, back) + sine(8, back)], 1)]
+        imag = [jnp.concatenate([first, cosine(8, back) - sine(7, back)], 1)]
+    for one in (1, 2, 3):
+        real.append(cosine(one) + sine(3 + one))
+        imag.append(cosine(3 + one) - sine(one))
+    return real + imag
+
+
+def rows_store(slots, target, offset):
+    for place in range(0, 8, 2):
+        both = jnp.concatenate([slots[place], slots[place + 1]], 0)
+        target[:, :, offset + 64 * place : offset + 64 * place + 128] = both.T.reshape(32, 8, 128)
+
+
+def rows_derived(slots, deriv):
+    out = [None] * 8
+    for one in range(4):
+        wave = deriv[one : one + 1, :]
+        out[one] = -wave * slots[4 + one]
+        out[4 + one] = wave * slots[one]
+    return out
+
+
+def rows_loaded(source, offset):
+    out = []
+    for place in range(0, 8, 2):
+        both = source[:, :, offset + 64 * place : offset + 64 * place + 128]
+        both = both.reshape(256, 128).T
+        out += [both[:64], both[64:]]
+    return out
+
+
+def put(high, low, place, value):
+    top, bottom = split_of(value)
+    high[64 * place : 64 * place + 64, :] = top
+    low[64 * place : 64 * place + 64, :] = bottom
+
+
+def eight_inverse(even, odd, ones, twos, threes, store):
+    root = math.sqrt(0.5)
+    plus, minus = even + odd, even - odd
+    back = root * (ones[0] - ones[1]) - root * (threes[0] + threes[1])
+    fore = root * (threes[0] - threes[1]) - root * (ones[0] + ones[1])
+    parts = (
+        (plus + twos[0], ones[0] + threes[0]),
+        (minus - twos[1], back),
+        (plus - twos[0], threes[1] - ones[1]),
+        (minus + twos[1], fore),
+    )
+    for one in range(4):
+        store(one, parts[one][0] + parts[one][1])
+        store(one + 4, parts[one][0] - parts[one][1])
+
+
+def rows_inverse(slots, high, low, product, pair, even, odd, spin, store):
+    for one in (1, 2, 3):
+        put(high, low, one - 1, slots[one])
+        put(high, low, 2 + one, slots[4 + one])
+    front, back = slice(0, 128), slice(128, 256)
+    put(high, low, 6, jnp.concatenate([slots[0][:, front], slots[4][:, front]], 1))
+    put(high, low, 7, jnp.concatenate([slots[0][:, back], slots[4][:, back]], 1))
+    product[0:384, :] = dots(high[0:384, :], low[0:384, :], pair[0][...], pair[1][...])
+    product[384:448, 0:256] = dots(high[384:448, :], low[384:448, :], even[0][...], even[1][...])
+    product[384:448, 256:512] = dots(high[448:512, :], low[448:512, :], odd[0][...], odd[1][...])
+    for row in range(0, 64, 16):
+        for lane in range(0, 256, 128):
+            turned = []
+            for one in (1, 2, 3):
+                at = slice(64 * (one - 1) + row, 64 * (one - 1) + row + 16)
+                to = slice(64 * (2 + one) + row, 64 * (2 + one) + row + 16)
+                lanes, moved = slice(lane, lane + 128), slice(lane + 256, lane + 384)
+                value = (
+                    product[at, lanes] - product[to, moved],
+                    product[to, lanes] + product[at, moved],
+                )
+                value = turn(
+                    value,
+                    2.0 * spin[0][one : one + 1, lanes],
+                    2.0 * spin[1][one : one + 1, lanes],
+                )
+                turned.append(value)
+            at = slice(384 + row, 400 + row)
+            eight_inverse(
+                product[at, lane : lane + 128],
+                product[at, lane + 256 : lane + 384],
+                *turned,
+                lambda one, value: store(one, slice(row, row + 16), slice(lane, lane + 128), value),
+            )
+
+
+def rows_whole(source, offset, high, low, product, pair, spin, store):
+    for place in range(0, 16, 2):
+        both = source[:, :, offset + 64 * place : offset + 64 * place + 128]
+        both = both.reshape(256, 128).T
+        top, bottom = split_of(both)
+        high[64 * place : 64 * place + 128, :] = top
+        low[64 * place : 64 * place + 128, :] = bottom
+    product[...] = dots(high[...], low[...], pair[0][...], pair[1][...])
+    for row in range(0, 64, 16):
+        for lane in range(0, 256, 128):
+            lanes, moved = slice(lane, lane + 128), slice(lane + 256, lane + 384)
+            turned = []
+            for one in range(8):
+                at = slice(64 * one + row, 64 * one + row + 16)
+                to = slice(512 + 64 * one + row, 512 + 64 * one + row + 16)
+                value = (
+                    product[at, lanes] - product[to, moved],
+                    product[to, lanes] + product[at, moved],
+                )
+                turned.append(
+                    turn(value, spin[0][one : one + 1, lanes], spin[1][one : one + 1, lanes])
+                )
+            joint = [
+                (turned[one][0] + turned[8 - one][0], turned[one][1] - turned[8 - one][1])
+                for one in (1, 2, 3)
+            ]
+            eight_inverse(
+                turned[0][0],
+                turned[4][0],
+                *joint,
+                lambda one, value: store(one, slice(row, row + 16), slice(lane, lane + 128), value),
+            )
+
+
+def put_tiles(high, low, place, first, second, lanes):
+    top, bottom = split_of(jnp.concatenate([first, second], 0))
+    high[8 * place : 8 * place + 16, lanes] = top
+    low[8 * place : 8 * place + 16, lanes] = bottom
+
+
+def cols_forward(source, offset, high, low, product, pair, spin):
+    for lane in range(0, 256, 128):
+        lanes = slice(lane, lane + 128)
+        values = [
+            (
+                source[one, :, offset + lane : offset + lane + 128],
+                source[one, :, offset + 256 + lane : offset + 384 + lane],
+            )
+            for one in range(32)
+        ]
+        values = butterflies(values, -1)
+        for one in range(32):
+            values[one] = turn(
+                values[one], spin[0][one : one + 1, lanes], -spin[1][one : one + 1, lanes]
+            )
+        for one in range(0, 32, 2):
+            put_tiles(high, low, one, values[one][0], values[one + 1][0], lanes)
+            put_tiles(high, low, 32 + one, values[one][1], values[one + 1][1], lanes)
+    product[0:512, :] = dots(high[0:512, :], low[0:512, :], pair[0][...], pair[1][...])
+
+    def tile(one, lanes=slice(0, 256)):
+        at, to = slice(8 * one, 8 * one + 8), slice(256 + 8 * one, 264 + 8 * one)
+        moved = slice(lanes.start + 256, lanes.stop + 256)
+        return (
+            product[at, lanes] + product[to, moved],
+            product[to, lanes] - product[at, moved],
+        )
+
+    return tile
+
+
+def cols_inverse(tile, high, low, product, pair, spin, target, offset, count=1):
+    for group in range(count):
+        for one in range(0, 32, 2):
+            first, second = tile(one, group), tile(one + 1, group)
+            put_tiles(high, low, one, first[0], second[0], slice(0, 256))
+            put_tiles(high, low, 32 + one, first[1], second[1], slice(0, 256))
+        product[0:512, :] = dots(high[0:512, :], low[0:512, :], pair[0][...], pair[1][...])
+        for lane in range(0, 256, 128):
+            lanes, moved = slice(lane, lane + 128), slice(lane + 256, lane + 384)
+            values = []
+            for one in range(32):
+                at, to = slice(8 * one, 8 * one + 8), slice(256 + 8 * one, 264 + 8 * one)
+                value = (
+                    product[at, lanes] - product[to, moved],
+                    product[to, lanes] + product[at, moved],
+                )
+                values.append(
+                    turn(value, spin[0][one : one + 1, lanes], spin[1][one : one + 1, lanes])
+                )
+            values = butterflies(values, 1)
+            for one in range(32):
+                at = offset + 256 * group + lane
+                target[one, :, at : at + 128] = values[one][0]
+                at += 256 * count
+                target[one, :, at : at + 128] = values[one][1]
+
+
+def mirrored(tile, one):
+    real, imag = tile((32 - one) % 32)
+    lane = lax.broadcasted_iota(jnp.int32, (8, 128), 1)
+    spot = jnp.where(lane < 64, (64 - lane) % 64 if one == 0 else 63 - lane, lane)
+    return (
+        jnp.take_along_axis(real, spot, axis=1),
+        -jnp.take_along_axis(imag, spot, axis=1),
+    )
+
+
+def kernel_start(field, ph, pl_, sc, ss, out, high, low, product):
+    def load(one, rows, lanes):
+        return field[rows, 256 * one + lanes.start : 256 * one + lanes.stop]
+
+    slots = rows_forward(load, high, low, product, (ph, pl_), (sc, ss), False)
+    rows_store(slots, out, 0)
+
+
+def kernel_slope(field, ph, pl_, eh, el, oh, ol, sc, ss, deriv, out, high, low, product):
+    def load(one, rows, lanes):
+        return field[rows, 256 * one + lanes.start : 256 * one + lanes.stop]
+
+    def store(one, rows, lanes, value):
+        out[rows, 256 * one + lanes.start : 256 * one + lanes.stop] = value
+
+    slots = rows_forward(load, high, low, product, (ph, pl_), (sc, ss), False)
+    slots = rows_derived(slots, deriv)
+    rows_inverse(
+        slots, high, low, product, (ph, pl_), (eh, el), (oh, ol), (sc, ss), store
+    )
+
+
+def kernel_force(force, ch, cl, tc, ts, out, mixed, turned, spec, high, low, product):
+    for lane in range(0, 2048, 128):
+        both = jnp.concatenate([force[part, :, lane : lane + 128] for part in range(2)], 0)
+        turned[lane : lane + 128, :] = both.T
+    lane = lax.broadcasted_iota(jnp.int32, (8, 128), 1)
+    for one in range(0, 32, 2):
+        both = jnp.concatenate(
+            [turned[pl.ds(one, 64, stride=32), :], turned[pl.ds(one + 1, 64, stride=32), :]], 0
+        ).T
+        base = 64 * one
+        mixed[base : base + 128, :] = both
+        for part in range(2):
+            for kind in range(0, 8, 2):
+                at = base + 64 * part + kind
+                first = mixed[pl.ds(at, 8, stride=8), :]
+                second = mixed[pl.ds(at + 1, 8, stride=8), :]
+                lanes = slice(512 * part + 64 * kind, 512 * part + 64 * kind + 128)
+                spec[8 * one : 8 * one + 8, lanes] = jnp.where(
+                    lane < 64, first, pltpu.roll(second, 64, 1)
+                )
+                spec[8 * one + 8 : 8 * one + 16, lanes] = jnp.where(
+                    lane < 64, pltpu.roll(first, 64, 1), second
+                )
+
+    def tile(one, group):
+        rows = slice(8 * one, 8 * one + 8)
+        return (
+            spec[rows, 256 * group : 256 * group + 256],
+            spec[rows, 512 + 256 * group : 768 + 256 * group],
+        )
+
+    cols_inverse(tile, high, low, product, (ch, cl), (tc, ts), out, 0, 2)
+
+
+def kernel_first(source, other, ch, cl, tc, ts, deriv, state, out, high, low, product):
+    tile = cols_forward(source, 0, high, low, product, (ch, cl), (tc, ts))
+    for one in range(32):
+        rows = slice(8 * one, 8 * one + 8)
+        real, imag = tile(one)
+        state[0, rows, :] = real
+        state[1, rows, :] = imag
+
+    def slope(one, group):
+        rows = slice(8 * one, 8 * one + 8)
+        wave = deriv[one : one + 1, :]
+        return -wave * state[1, rows, :], wave * state[0, rows, :]
+
+    cols_inverse(slope, high, low, product, (ch, cl), (tc, ts), out, 0)
+    out[:, :, 512:1536] = other[...]
+
+
+def kernel_bend(
+    source, second, other, ph, pl_, eh, el, oh, ol, sc, ss, grad, out, bend, high, low, product
+):
+    def put_bend(one, rows, lanes, value):
+        bend[rows, 256 * one + lanes.start : 256 * one + lanes.stop] = value
+
+    rows_whole(source, 512, high, low, product, (ph, pl_), (sc, ss), put_bend)
+
+    def store(one, rows, lanes, value):
+        to = slice(256 * one + lanes.start, 256 * one + lanes.stop)
+        grad[rows, to] = value
+        side = second[rows, to]
+        bend[rows, to] = bend[rows, to] - 0.5 * (value * value + side * side)
+
+    slots = rows_loaded(source, 0)
+    rows_inverse(slots, high, low, product, (ph, pl_), (eh, el), (oh, ol), (sc, ss), store)
+
+    def load(one, rows, lanes):
+        return bend[rows, 256 * one + lanes.start : 256 * one + lanes.stop]
+
+    slots = rows_forward(load, high, low, product, (ph, pl_), (sc, ss), False)
+    rows_store(slots, out, 0)
+    out[:, :, 512:1024] = other[...]
+
+
+def kernel_solve(
+    source, state, damp, cross, ch, cl, tc, ts, coef, out, goal, fresh, high, low, product
+):
+    tile = cols_forward(source, 512, high, low, product, (ch, cl), (tc, ts))
+    for one in range(32):
+        rows = slice(8 * one, 8 * one + 8)
+        goal[0, rows, :], goal[1, rows, :] = tile(one)
+    tile = cols_forward(source, 0, high, low, product, (ch, cl), (tc, ts))
+    for one in range(32):
+        rows = slice(8 * one, 8 * one + 8)
+        real, imag = tile(one)
+        fresh[0, rows, :] = state[0, rows, :] + time_step * real
+        fresh[1, rows, :] = state[1, rows, :] + time_step * imag
+
+    def front(array):
+        def view(one):
+            rows = slice(8 * one, 8 * one + 8)
+            return array[0, rows, 0:128], array[1, rows, 0:128]
+
+        return view
+
+    def damped(value, flipped, one):
+        rows = slice(8 * one, 8 * one + 8)
+        weight, mixed = damp[rows, :], cross[rows, :]
+        return tuple(
+            jnp.concatenate(
+                [
+                    value[part][:, 0:128] * weight[:, 0:128] + flipped[part] * mixed,
+                    value[part][:, 128:256] * weight[:, 128:256],
+                ],
+                1,
+            )
+            for part in range(2)
+        )
+
+    held = []
+    for one in range(32):
+        rows = slice(8 * one, 8 * one + 8)
+        value = (fresh[0, rows, :], fresh[1, rows, :])
+        flipped = mirrored(front(fresh), one)
+        following = damped(value, flipped, one)
+        weight, mixed = damp[rows, 0:128], cross[rows, :]
+        back = mirrored(front(goal), one)
+        turned_back = tuple(
+            flipped[part] * weight + value[part][:, 0:128] * mixed - back[part]
+            for part in range(2)
+        )
+        miss = tuple(following[part] - goal[part, rows, :] for part in range(2))
+        slope = damped(miss, turned_back, one)
+        for part in range(2):
+            coef[part, rows, :] = time_step * slope[part]
+            goal_next = following[part]
+            product[256 * part + 8 * one : 256 * part + 8 * one + 8, 0:256] = goal_next
+    for part in range(2):
+        fresh[part, :, :] = product[256 * part : 256 * part + 256, 0:256]
+
+    def scaled(one, group):
+        rows = slice(8 * one, 8 * one + 8)
+        return coef[0, rows, :], coef[1, rows, :]
+
+    def following_tile(one, group):
+        rows = slice(8 * one, 8 * one + 8)
+        return fresh[0, rows, :], fresh[1, rows, :]
+
+    cols_inverse(scaled, high, low, product, (ch, cl), (tc, ts), out, 0)
+    cols_inverse(following_tile, high, low, product, (ch, cl), (tc, ts), out, 512)
+
+
+def kernel_adjoint(
+    source, grad, ph, pl_, eh, el, oh, ol, sc, ss, mult, out, joint, high, low, product
+):
+    def store(one, rows, lanes, value):
+        to = slice(256 * one + lanes.start, 256 * one + lanes.stop)
+        mult[rows, to] = value
+        joint[rows, to] = value * grad[rows, to]
+
+    slots = rows_loaded(source, 0)
+    rows_inverse(slots, high, low, product, (ph, pl_), (eh, el), (oh, ol), (sc, ss), store)
+
+    def load(one, rows, lanes):
+        return joint[rows, 256 * one + lanes.start : 256 * one + lanes.stop]
+
+    slots = rows_forward(load, high, low, product, (ph, pl_), (sc, ss), False)
+    rows_store(slots, out, 0)
+
+    def load_other(one, rows, lanes):
+        return mult[rows, 256 * one + lanes.start : 256 * one + lanes.stop]
+
+    slots = rows_forward(load_other, high, low, product, (ph, pl_), (sc, ss), True)
+    rows_store(slots, out, 512)
+
+
+def kernel_side(
+    source, goal, mult, second, ph, pl_, eh, el, oh, ol, sc, ss, deriv,
+    ahead, side, miss, joint, high, low, product,
+):
+    def store(one, rows, lanes, value):
+        to = slice(256 * one + lanes.start, 256 * one + lanes.stop)
+        ahead[rows, to] = value
+        joint[rows, to] = mult[rows, to] * second[rows, to]
+
+    slots = rows_loaded(source, 512)
+    rows_inverse(slots, high, low, product, (ph, pl_), (eh, el), (oh, ol), (sc, ss), store)
+    total = jnp.zeros((8, 256), jnp.float32)
+    for row in range(0, 64, 8):
+        for lane in range(0, 2048, 256):
+            gap = ahead[row : row + 8, lane : lane + 256] - goal[row : row + 8, lane : lane + 256]
+            total = total + gap * gap
+    miss[...] = jnp.broadcast_to(0.5 * jnp.sum(total), (8, 128))
+
+    def load(one, rows, lanes):
+        return joint[rows, 256 * one + lanes.start : 256 * one + lanes.stop]
+
+    slots = rows_forward(load, high, low, product, (ph, pl_), (sc, ss), False)
+    slots = rows_derived(slots, deriv)
+    for place in range(8):
+        side[64 * place : 64 * place + 64, :] = slots[place]
+
+
+def kernel_last(source, coef, miss, ch, cl, tc, ts, deriv, out, spec, high, low, product):
+    tile = cols_forward(source, 0, high, low, product, (ch, cl), (tc, ts))
+    for one in range(32):
+        rows = slice(8 * one, 8 * one + 8)
+        real, imag = tile(one)
+        wave = deriv[one : one + 1, :]
+        spec[0, rows, :] = coef[0, rows, :] * (1.0 / time_step) - wave * imag
+        spec[1, rows, :] = coef[1, rows, :] * (1.0 / time_step) + wave * real
+
+    def whole(one, group):
+        rows = slice(8 * one, 8 * one + 8)
+        return spec[0, rows, :], spec[1, rows, :]
+
+    cols_inverse(whole, high, low, product, (ch, cl), (tc, ts), out, 0)
+    out[:, :, 512:640] = jnp.broadcast_to(miss[...][None], (32, 8, 128))
+
+
+def kernel_force_grad(
+    place, source, coef, ch, cl, tc, ts, out, mixed, turned, high, low, product
+):
+    tile = cols_forward(source, 512, high, low, product, (ch, cl), (tc, ts))
+    early = place[0] < 16
+    corner = place[0] == 0
+    lane = lax.broadcasted_iota(jnp.int32, (8, 128), 1)
+    row = lax.broadcasted_iota(jnp.int32, (8, 128), 0)
+    packed = jnp.logical_and(jnp.logical_and(row == 0, lane < 64), corner)
+
+    def front(one):
+        rows = slice(8 * one, 8 * one + 8)
+        return coef[0, rows, 0:128], coef[1, rows, 0:128]
+
+    def lanes_of(one):
+        rows = slice(8 * one, 8 * one + 8)
+        far = tile(one)
+        flipped = mirrored(front, one)
+        out_parts = []
+        for part in range(2):
+            near_front = coef[part, rows, 0:128]
+            near_front = jnp.where(packed, 0.5 * (near_front + flipped[part]), near_front)
+            near_back = coef[part, rows, 128:256]
+            far_front, far_back = far[part][:, 0:128], far[part][:, 128:256]
+            low_half = lane < 64
+            swap = jnp.logical_and(low_half, jnp.logical_not(early))
+            out_parts.append(
+                [
+                    jnp.where(swap, far_front, near_front),
+                    near_back,
+                    jnp.where(swap, near_front, far_front),
+                    far_back,
+                ]
+            )
+        return out_parts
+
+    for one in range(0, 32, 2):
+        first, second = lanes_of(one), lanes_of(one + 1)
+        base = 64 * one
+        for part in range(2):
+            for pairs in range(4):
+                left, right = first[part][pairs], second[part][pairs]
+                at = base + 64 * part + 2 * pairs
+                mixed[pl.ds(at, 8, stride=8), :] = jnp.where(
+                    lane < 64, left, pltpu.roll(right, 64, 1)
+                )
+                mixed[pl.ds(at + 1, 8, stride=8), :] = jnp.where(
+                    lane < 64, pltpu.roll(left, 64, 1), right
+                )
+        both = mixed[base : base + 128, :].T
+        turned[pl.ds(one, 64, stride=32), :] = both[:64]
+        turned[pl.ds(one + 1, 64, stride=32), :] = both[64:]
+    for start in range(0, 2048, 128):
+        both = turned[start : start + 128, :].T
+        for part in range(2):
+            out[part, :, start : start + 128] = both[64 * part : 64 * part + 64]
+
+
+def kernel_finish(source, side, ph, pl_, eh, el, oh, ol, sc, ss, out, total, high, low, product):
+    slots = rows_loaded(source, 0)
+    slots = [slots[place] + side[64 * place : 64 * place + 64, :] for place in range(8)]
+
+    def store(one, rows, lanes, value):
+        out[rows, 256 * one + lanes.start : 256 * one + lanes.stop] = value
+
+    rows_inverse(slots, high, low, product, (ph, pl_), (eh, el), (oh, ol), (sc, ss), store)
+    total[...] = jnp.sum(source[:, :, 512:640], axis=0)
+
+
+def call(body, outputs, scratch, *operands, scalars=0):
+    specs = [pl.BlockSpec(memory_space=pltpu.SMEM)] * scalars
+    specs += [pl.BlockSpec(memory_space=pltpu.VMEM)] * (len(operands) - scalars)
+    return pl.pallas_call(
+        body,
+        out_shape=tuple(jax.ShapeDtypeStruct(one, jnp.float32) for one in outputs),
+        in_specs=specs,
+        out_specs=tuple(pl.BlockSpec(memory_space=pltpu.VMEM) for _ in outputs),
+        scratch_shapes=scratch,
+        name=body.__name__,
+        compiler_params=pltpu.CompilerParams(vmem_limit_bytes=48 * 2**20),
+    )(*operands)
+
+
+def work(rows):
+    return [
+        pltpu.VMEM((rows, 256), jnp.bfloat16),
+        pltpu.VMEM((rows, 256), jnp.bfloat16),
+        pltpu.VMEM((rows, 512), jnp.float32),
+    ]
+
+
+def exchange(value):
+    return lax.all_to_all(value, ("px", "py"), split_axis=0, concat_axis=0, tiled=True)
+
+
+def per_device_fast(initial_field, target_field, forcing):
+    length = initial_field.shape[2]
+    local = initial_field.shape[1]
+    parts = length // local
+    device = lax.axis_index(("px", "py"))
+    tables = Tables(length, parts)
+    inner = length // 8
+    field, goal = initial_field[0], target_field[0]
+    rows_all = tables.row_pair + tables.even_pair + tables.odd_pair + tables.row_turn
+    rows_some = tables.row_pair + tables.row_turn
+    cols = tables.col_pair + tables.col_turn
+    f32 = jnp.float32
+    own = jnp.arange(8, dtype=jnp.int32)[None, :, None]
+    kind = jnp.arange(inner, dtype=jnp.int32)[None, None, :] // local
+    late = jnp.where(device < parts // 2, 0, 4)
+    second = device * local + 8 * own + jnp.where(kind == 0, late, kind)
+    wave_first = jnp.asarray(tables.col_wave, f32)[:, None, :]
+
+    def inverse_of(index):
+        wave = waves_of(index, length)[0]
+        square = wave_first * wave_first + wave * wave
+        return 1.0 / (1.0 + time_step * (square * square - square))
+
+    packed = (second == 0) & (kind == 0)
+    plain = inverse_of(second)
+    middle = inverse_of(second + length // 2)
+    damp = jnp.where(packed, 0.5 * (plain + middle), plain).reshape(inner, inner)
+    cross = jnp.where(packed, 0.5 * (plain - middle), 0.0).reshape(inner, inner)[:, :128]
+
+    block = (parts, 8, 512)
+    (sent,) = call(kernel_start, [block], work(576), field, *rows_some)
+    first = exchange(sent)
+    (force,) = call(
+        kernel_force,
+        [(parts, 8, 1024)],
+        [pltpu.VMEM((length, 128), f32), pltpu.VMEM((length, 128), f32), pltpu.VMEM((256, 1024), f32)]
+        + work(512),
+        forcing,
+        *cols,
+    )
+    (goal_rows,) = call(kernel_start, [block], work(576), goal, *rows_some)
+    (grad_second,) = call(
+        kernel_slope, [(local, length)], work(576), field, *rows_all, tables.row_deriv
+    )
+    state, sent = call(
+        kernel_first,
+        [(2, 256, 256), (parts, 8, 1536)],
+        work(512),
+        first,
+        force,
+        *cols,
+        tables.col_deriv,
+    )
+    moved = exchange(sent)
+    grad_first, sent = call(
+        kernel_bend,
+        [(local, length), (parts, 8, 1024)],
+        [pltpu.VMEM((local, length), f32)] + work(1024),
+        moved,
+        grad_second,
+        goal_rows,
+        *rows_all,
+    )
+    moved = exchange(sent)
+    coef, sent = call(
+        kernel_solve,
+        [(2, 256, 256), (parts, 8, 1024)],
+        [pltpu.VMEM((2, 256, 256), f32), pltpu.VMEM((2, 256, 256), f32)] + work(512),
+        moved,
+        state,
+        damp,
+        cross,
+        *cols,
+    )
+    moved = exchange(sent)
+    mult, sent = call(
+        kernel_adjoint,
+        [(local, length), (parts, 8, 1024)],
+        [pltpu.VMEM((local, length), f32)] + work(576),
+        moved,
+        grad_first,
+        *rows_all,
+    )
+    next_field, side, miss = call(
+        kernel_side,
+        [(local, length), (512, 256), (8, 128)],
+        [pltpu.VMEM((local, length), f32)] + work(576),
+        moved,
+        goal,
+        mult,
+        grad_second,
+        *rows_all,
+        tables.row_deriv,
+    )
+    moved = exchange(sent)
+    (sent,) = call(
+        kernel_last,
+        [(parts, 8, 640)],
+        [pltpu.VMEM((2, 256, 256), f32)] + work(512),
+        moved,
+        coef,
+        miss,
+        *cols,
+        tables.col_deriv,
+    )
+    (forcing_grad,) = call(
+        kernel_force_grad,
+        [(2, local, length)],
+        [pltpu.VMEM((length, 128), f32), pltpu.VMEM((length, 128), f32)] + work(512),
+        jnp.asarray(device, jnp.int32).reshape(1),
+        moved,
+        coef,
+        *cols,
+        scalars=1,
+    )
+    moved = exchange(sent)
+    field_grad, total = call(
+        kernel_finish, [(local, length), (8, 128)], work(576), moved, side, *rows_all
+    )
+    objective = total[0, 0] / (length * length)
+    return (next_field[None], objective, field_grad[None], forcing_grad)
+
+
+def fits(initial_field, forcing):
+    members, local, length = initial_field.shape
+    return (
+        members == 1
+        and forcing.shape[1] == local
+        and forcing.shape[2] == length
+        and local == 64
+        and length == 32 * local
+    )
+
+
+def per_device(initial_field, target_field, forcing):
+    if fits(initial_field, forcing):
+        return per_device_fast(initial_field, target_field, forcing)
+    return per_device_plain(initial_field, target_field, forcing)
+
+
 def solution(mesh):
     return jax.shard_map(
         per_device,

time: 894 us -> 214 us (0.24); the launches traced: 883 us -> 213 us
  matrix products: 321 us -> 0 us
  other arithmetic: 217 us -> 0.35 us
  local copies, waits for them, and re-layouts: 176 us -> 27.1 us
  waiting for transfers between devices: 40.4 us -> 105 us
  starting transfers between devices: 83.1 us -> 21.5 us
  Pallas kernels: 0 us -> 26.8 us
  blocking collectives: 40.5 us -> 29.6 us
    dot_general x116 -> x0, matrix products: 321 us -> none  [the longest x29 81.2 us: complex_einsum(): imag_term = jnp.einsum(formula, left_real, table_pair[1], precision=highest)]
    unnamed x16 -> x0, other arithmetic: 167 us -> none
    all_to_all x16 -> x5, waiting for transfers between devices: 40.4 us -> 105 us  [exchange(): lax.all_to_all(value, ('px', 'py'), split_axis=0, concat_axis=0, tiled=True)]
    all_to_all x16 -> x5, starting transfers between devices: 83.1 us -> 21.5 us  [exchange(): lax.all_to_all(value, ('px', 'py'), split_axis=0, concat_axis=0, tiled=True)]
    unnamed x115 -> x114, local copies, waits for them, and re-layouts: 74.6 us -> 26.5 us
    all_to_all x16 -> x0, other arithmetic: 40.7 us -> none  [the longest x8 20.9 us: regroup(): lax.all_to_all(real_part, ('px', 'py'), split_axis=2, concat_axis=1, tile...]
    psum x1 -> x0, blocking collectives: 40.5 us -> none  [per_device(): total = lax.psum(0.5 * jnp.sum(residual * residual), ('px', 'py'))]
    all_to_all x0 -> x1, blocking collectives: none -> 29.6 us  [exchange(): lax.all_to_all(value, ('px', 'py'), split_axis=0, concat_axis=0, tiled=True)]
  transfers between devices with their start and end apart: 16 -> 5, of which waited for: 8 -> 5; matrix products, arithmetic and copies ran while one was open for 28% -> 0% of each run, Pallas kernels for 0% -> 5%
where the time goes in v1:
time: 214 us; the launch traced here: 213 us
  waiting for transfers between devices  105 us (49%)
  blocking collectives  29.6 us (14%)
  local copies, waits for them, and re-layouts  27.1 us (13%)
  Pallas kernels  26.8 us (13%)
  starting transfers between devices  21.5 us (10%)
  between operations  2.88 us (1%)
    all_to_all x5, waiting for transfers between devices, exchange(): lax.all_to_all(value, ('px', 'py'), split_axis=0, concat_axis=0, tiled=True)  105 us
    all_to_all x1, blocking collectives, exchange(): lax.all_to_all(value, ('px', 'py'), split_axis=0, concat_axis=0, tiled=True)  29.6 us
    pallas_call x12, Pallas kernels, call(): pl.pallas_call(body, out_shape=tuple((jax.ShapeDtypeStruct(one, jnp.float...  26.8 us
    unnamed x114, local copies, waits for them, and re-layouts  26.5 us
    all_to_all x5, starting transfers between devices, exchange(): lax.all_to_all(value, ('px', 'py'), split_axis=0, concat_axis=0, tiled=True)  21.5 us
  transfers between devices with their start and end apart: 5, of which 5 were waited for; matrix products, arithmetic and copies ran while one was open for 0% of the time, Pallas kernels for 5%

profile of v1, /device:TPU:0, one launch (start us, length us, event | category | flops | bytes accessed | tf_op | source)
XLA Modules:
  0.0 212.8 jit_solution(9542620242793046162)
XLA Ops:
  5.0 1.7 kernel_start.2
  6.7 7.3 %all-to-all-start = ((f32[32,8,512]{2,1,0:T(8,128)}), f32[32,8,512]{2,1,0:T(8,128)S(1)}, u32[]{:S(2)}, u32[]{:S(2)}) async-start(f32[32,8,512]{2,1,0:T(8,128)} %kernel_start.2), calls=%async_computation | async-start | bytes 1048576 | tf_op jit(solution)/shard_map/all_to_all | solution.py:828
  14.1 2.4 %kernel_force.1.other = f32[32,8,1024]{2,1,0:T(8,128)S(1)} custom-call(f32[2,64,2048]{2,1,0:T(8,128)S(1)} %copy-done.29, bf16[256,512]{1,0:T(8,128)(2,1)S(1)} %copy-done.4, bf16[256,512]{1,0:T(8,128)(2,1)S(1)} %copy-done.5, f32[32,256]{1,0:T(8,128)S(1)} %copy-done.30, f32[32,256]{1,0:T(8,128)S(1)} %copy-done.34), custom_call_target="tpu_custom_call" | custom-call | tf_op jit(solution)/shard_map/kernel_force/pallas_call | solution.py:808
  16.5 13.1 %all-to-all-done.source = f32[32,8,512]{2,1,0:T(8,128)S(1)} async-done(((f32[32,8,512]{2,1,0:T(8,128)}), f32[32,8,512]{2,1,0:T(8,128)S(1)}, u32[]{:S(2)}, u32[]{:S(2)}) %all-to-all-start) | async-done | bytes 524320 | tf_op jit(solution)/shard_map/all_to_all | solution.py:828
  29.6 2.1 %kernel_first.1 = (f32[2,256,256]{2,1,0:T(8,128)S(1)}, f32[32,8,1536]{2,1,0:T(8,128)S(1)}) custom-call(f32[32,8,512]{2,1,0:T(8,128)S(1)} %all-to-all-done.source, f32[32,8,1024]{2,1,0:T(8,128)S(1)} %kernel_force.1.other, bf16[256,512]{1,0:T(8,128)(2,1)S(1)} %copy-done.4, bf16[256,512]{1,0:T(8,128)(2,1)S(1)} %copy-done.5, f32[32,256]{1,0:T(8,128)S(1)} %copy-done.30, ...), custom_call_target="tpu_custom_call" | custom-call | tf_op jit(solution)/shard_map/kernel_first/pallas_call | solution.py:808
  31.8 1.2 copy-done.26
  33.8 3.0 %all-to-all-start.1 = ((f32[32,8,1536]{2,1,0:T(8,128)}), f32[32,8,1536]{2,1,0:T(8,128)S(1)}, u32[]{:S(2)}, u32[]{:S(2)}) async-start(f32[32,8,1536]{2,1,0:T(8,128)} %copy-done.26), calls=%async_computation.1 | async-start | bytes 3145728 | tf_op jit(solution)/shard_map/all_to_all | solution.py:828
  38.6 1.9 kernel_slope.1.second
  40.6 33.9 %all-to-all-done.1.source = f32[32,8,1536]{2,1,0:T(8,128)S(1)} async-done(((f32[32,8,1536]{2,1,0:T(8,128)}), f32[32,8,1536]{2,1,0:T(8,128)S(1)}, u32[]{:S(2)}, u32[]{:S(2)}) %all-to-all-start.1) | async-done | bytes 1572896 | tf_op jit(solution)/shard_map/all_to_all | solution.py:828
  76.4 3.5 %kernel_bend.1 = (f32[64,2048]{1,0:T(8,128)S(1)}, f32[32,8,1024]{2,1,0:T(8,128)S(1)}) custom-call(f32[32,8,1536]{2,1,0:T(8,128)S(1)} %all-to-all-done.1.source, f32[64,2048]{1,0:T(8,128)S(1)} %kernel_slope.1.second, f32[32,8,512]{2,1,0:T(8,128)S(1)} %copy-done.18, bf16[256,512]{1,0:T(8,128)(2,1)S(1)} %copy-done.1, bf16[256,512]{1,0:T(8,128)(2,1)S(1)} %copy-done.3, ...), custom_call_target="tpu_custom_call" | custom-call | tf_op jit(solution)/shard_map/kernel_bend/pallas_call | solution.py:808
  81.7 4.0 %all-to-all-start.2 = ((f32[32,8,1024]{2,1,0:T(8,128)}), f32[32,8,1024]{2,1,0:T(8,128)S(1)}, u32[]{:S(2)}, u32[]{:S(2)}) async-start(f32[32,8,1024]{2,1,0:T(8,128)} %copy-done.27), calls=%async_computation.2 | async-start | bytes 2097152 | tf_op jit(solution)/shard_map/all_to_all | solution.py:828
  86.1 25.6 %all-to-all-done.2.source = f32[32,8,1024]{2,1,0:T(8,128)S(1)} async-done(((f32[32,8,1024]{2,1,0:T(8,128)}), f32[32,8,1024]{2,1,0:T(8,128)S(1)}, u32[]{:S(2)}, u32[]{:S(2)}) %all-to-all-start.2) | async-done | bytes 1048608 | tf_op jit(solution)/shard_map/all_to_all | solution.py:828
  111.7 3.0 %kernel_solve.1 = (f32[2,256,256]{2,1,0:T(8,128)S(1)}, f32[32,8,1024]{2,1,0:T(8,128)S(1)}) custom-call(f32[32,8,1024]{2,1,0:T(8,128)S(1)} %all-to-all-done.2.source, f32[2,256,256]{2,1,0:T(8,128)S(1)} %copy-done.39, f32[256,256]{1,0:T(8,128)S(1)} %get-tuple-element.31.damp, f32[256,128]{1,0:T(8,128)S(1)} %fusion.7.cross, bf16[256,512]{1,0:T(8,128)(2,1)S(1)} %copy-done.4, ...), custom_call_target="tpu_custom_call" | custom-call | tf_op jit(solution)/shard_map/kernel_solve/pallas_call | solution.py:808
  115.5 29.6 %all_to_all.30.source = f32[32,8,1024]{2,1,0:T(8,128)S(1)} all-to-all(f32[32,8,1024]{2,1,0:T(8,128)S(1)} %get-tuple-element.20), channel_id=1, replica_groups=mesh['px'=8,'py'=4] {'px','py'}, dimensions={0} | all-to-all | bytes 2097152 | tf_op jit(solution)/shard_map/all_to_all | solution.py:828
  145.1 2.6 %kernel_adjoint.1 = (f32[64,2048]{1,0:T(8,128)S(1)}, f32[32,8,1024]{2,1,0:T(8,128)S(1)}) custom-call(f32[32,8,1024]{2,1,0:T(8,128)S(1)} %all_to_all.30.source, f32[64,2048]{1,0:T(8,128)S(1)} %copy-done.41, bf16[256,512]{1,0:T(8,128)(2,1)S(1)} %copy-done.1, bf16[256,512]{1,0:T(8,128)(2,1)S(1)} %copy-done.3, bf16[256,256]{1,0:T(8,128)(2,1)S(1)} %copy-done.8, ...), custom_call_target="tpu_custom_call" | custom-call | tf_op jit(solution)/shard_map/kernel_adjoint/pallas_call | solution.py:808
  149.5 3.6 %all-to-all-start.4 = ((f32[32,8,1024]{2,1,0:T(8,128)}), f32[32,8,1024]{2,1,0:T(8,128)S(1)}, u32[]{:S(2)}, u32[]{:S(2)}) async-start(f32[32,8,1024]{2,1,0:T(8,128)} %copy-done.28), calls=%async_computation.4 | async-start | bytes 2097152 | tf_op jit(solution)/shard_map/all_to_all | solution.py:828
  157.8 1.9 kernel_side.1
  161.1 18.2 %all-to-all-done.4.source = f32[32,8,1024]{2,1,0:T(8,128)S(1)} async-done(((f32[32,8,1024]{2,1,0:T(8,128)}), f32[32,8,1024]{2,1,0:T(8,128)S(1)}, u32[]{:S(2)}, u32[]{:S(2)}) %all-to-all-start.4) | async-done | bytes 1048608 | tf_op jit(solution)/shard_map/all_to_all | solution.py:828
  183.3 2.1 kernel_last.1
  186.3 3.6 %all-to-all-start.5 = ((f32[32,8,640]{2,1,0:T(8,128)}), f32[32,8,640]{2,1,0:T(8,128)S(1)}, u32[]{:S(2)}, u32[]{:S(2)}) async-start(f32[32,8,640]{2,1,0:T(8,128)} %copy-done.16), calls=%async_computation.5 | async-start | bytes 1310720 | tf_op jit(solution)/shard_map/all_to_all | solution.py:828
  191.0 3.1 %kernel_force_grad.1 = f32[2,64,2048]{2,1,0:T(8,128)} custom-call(s32[1]{0:T(128)} %bitcast.8.place, f32[32,8,1024]{2,1,0:T(8,128)S(1)} %all-to-all-done.4.source, f32[2,256,256]{2,1,0:T(8,128)S(1)} %copy-done.25, bf16[256,512]{1,0:T(8,128)(2,1)S(1)} %copy-done.4, bf16[256,512]{1,0:T(8,128)(2,1)S(1)} %copy-done.5, f32[32,256]{1,0:T(8,128)S(1)} %copy-done.33, ...), custom_call_target="tpu_custom_call" | custom-call | tf_op jit(solution)/shard_map/kernel_force_grad/pallas_call | solution.py:808
  194.1 13.8 %all-to-all-done.5.source = f32[32,8,640]{2,1,0:T(8,128)S(1)} async-done(((f32[32,8,640]{2,1,0:T(8,128)}), f32[32,8,640]{2,1,0:T(8,128)S(1)}, u32[]{:S(2)}, u32[]{:S(2)}) %all-to-all-start.5) | async-done | bytes 655392 | tf_op jit(solution)/shard_map/all_to_all | solution.py:828
  207.9 1.0 copy-done.43
  209.0 1.6 kernel_finish.1
  (122 shorter events, 26.0 us)
Async XLA Ops:
  0.6 13.4 %copy-start.30 = (f32[32,256]{1,0:T(8,128)S(1)}, f32[32,256]{1,0:T(8,128)}, u32[]{:S(2)}) copy-start(f32[32,256]{1,0:T(8,128)} %constant.106.clone.tc) | copy-start | bytes 98308
  5.0 9.0 %copy-start.4 = (bf16[256,512]{1,0:T(8,128)(2,1)S(1)}, bf16[256,512]{1,0:T(8,128)(2,1)}, u32[]{:S(2)}) copy-start(bf16[256,512]{1,0:T(8,128)(2,1)} %constant.104.clone.ch) | copy-start | bytes 786436
  5.0 9.0 %copy-start.5 = (bf16[256,512]{1,0:T(8,128)(2,1)S(1)}, bf16[256,512]{1,0:T(8,128)(2,1)}, u32[]{:S(2)}) copy-start(bf16[256,512]{1,0:T(8,128)(2,1)} %constant.105.clone.cl) | copy-start | bytes 786436
  5.0 9.1 %copy-start.29 = (f32[2,64,2048]{2,1,0:T(8,128)S(1)}, f32[2,64,2048]{2,1,0:T(8,128)}, u32[]{:S(2)}) copy-start(f32[2,64,2048]{2,1,0:T(8,128)} %force.1) | copy-start | bytes 3145732
  5.0 9.1 %copy-start.34 = (f32[32,256]{1,0:T(8,128)S(1)}, f32[32,256]{1,0:T(8,128)}, u32[]{:S(2)}) copy-start(f32[32,256]{1,0:T(8,128)} %constant.107.clone.ts) | copy-start | bytes 98308
  6.7 22.9 %all-to-all-start = ((f32[32,8,512]{2,1,0:T(8,128)}), f32[32,8,512]{2,1,0:T(8,128)S(1)}, u32[]{:S(2)}, u32[]{:S(2)}) async-start(f32[32,8,512]{2,1,0:T(8,128)} %kernel_start.2), calls=%async_computation | async-start | bytes 1048576 | tf_op jit(solution)/shard_map/all_to_all | solution.py:828
  14.1 15.6 %copy-start.50 = (f32[32,256]{1,0:T(8,128)S(1)}, f32[32,256]{1,0:T(8,128)}, u32[]{:S(2)}) copy-start(f32[32,256]{1,0:T(8,128)} %constant.108.clone.deriv) | copy-start | bytes 98308
  33.8 3.1 %copy-start.21 = (f32[1,64,2048]{2,1,0:T(8,128)S(1)}, f32[1,64,2048]{2,1,0:T(8,128)}, u32[]{:S(2)}) copy-start(f32[1,64,2048]{2,1,0:T(8,128)} %param.19) | copy-start | bytes 1572868
  33.8 3.1 %copy-start.47 = (f32[8,256]{1,0:T(8,128)S(1)}, f32[8,256]{1,0:T(8,128)}, u32[]{:S(2)}) copy-start(f32[8,256]{1,0:T(8,128)} %constant.98.clone.sc) | copy-start | bytes 24580
  33.8 3.1 %copy-start.49 = (f32[8,256]{1,0:T(8,128)S(1)}, f32[8,256]{1,0:T(8,128)}, u32[]{:S(2)}) copy-start(f32[8,256]{1,0:T(8,128)} %constant.99.clone.ss) | copy-start | bytes 24580
  33.8 40.6 %all-to-all-start.1 = ((f32[32,8,1536]{2,1,0:T(8,128)}), f32[32,8,1536]{2,1,0:T(8,128)S(1)}, u32[]{:S(2)}, u32[]{:S(2)}) async-start(f32[32,8,1536]{2,1,0:T(8,128)} %copy-done.26), calls=%async_computation.1 | async-start | bytes 3145728 | tf_op jit(solution)/shard_map/all_to_all | solution.py:828
  40.6 39.3 %copy-start.6 = (f32[64,2048]{1,0:T(8,128)}, f32[64,2048]{1,0:T(8,128)S(1)}, u32[]{:S(2)}) copy-start(f32[64,2048]{1,0:T(8,128)S(1)} %kernel_slope.1.second) | copy-start | bytes 1572868
  81.7 4.2 %copy-start.56 = (f32[32,256]{1,0:T(8,128)S(1)}, f32[32,256]{1,0:T(8,128)}, u32[]{:S(2)}) copy-start(f32[32,256]{1,0:T(8,128)} %constant.111) | copy-start | bytes 98308
  81.7 30.0 %copy-start.31 = (f32[32,256]{1,0:T(8,128)S(1)}, f32[32,256]{1,0:T(8,128)}, u32[]{:S(2)}) copy-start(f32[32,256]{1,0:T(8,128)} %constant.106.clone.tc) | copy-start | bytes 98308
  81.7 30.0 %copy-start.35 = (f32[32,256]{1,0:T(8,128)S(1)}, f32[32,256]{1,0:T(8,128)}, u32[]{:S(2)}) copy-start(f32[32,256]{1,0:T(8,128)} %constant.107.clone.ts) | copy-start | bytes 98308
  81.7 30.0 %copy-start.39 = (f32[2,256,256]{2,1,0:T(8,128)S(1)}, f32[2,256,256]{2,1,0:T(8,128)}, u32[]{:S(2)}) copy-start(f32[2,256,256]{2,1,0:T(8,128)} %copy-done.38) | copy-start | bytes 1572868
  81.7 30.0 %all-to-all-start.2 = ((f32[32,8,1024]{2,1,0:T(8,128)}), f32[32,8,1024]{2,1,0:T(8,128)S(1)}, u32[]{:S(2)}, u32[]{:S(2)}) async-start(f32[32,8,1024]{2,1,0:T(8,128)} %copy-done.27), calls=%async_computation.2 | async-start | bytes 2097152 | tf_op jit(solution)/shard_map/all_to_all | solution.py:828
  115.5 29.6 %copy-start.13 = (bf16[256,256]{1,0:T(8,128)(2,1)S(1)}, bf16[256,256]{1,0:T(8,128)(2,1)}, u32[]{:S(2)}) copy-start(bf16[256,256]{1,0:T(8,128)(2,1)} %constant.103.clone.ol) | copy-start | bytes 393220
  115.5 29.6 %copy-start.41 = (f32[64,2048]{1,0:T(8,128)S(1)}, f32[64,2048]{1,0:T(8,128)}, u32[]{:S(2)}) copy-start(f32[64,2048]{1,0:T(8,128)} %copy-done.40) | copy-start | bytes 1572868
  149.5 29.8 %all-to-all-start.4 = ((f32[32,8,1024]{2,1,0:T(8,128)}), f32[32,8,1024]{2,1,0:T(8,128)S(1)}, u32[]{:S(2)}, u32[]{:S(2)}) async-start(f32[32,8,1024]{2,1,0:T(8,128)} %copy-done.28), calls=%async_computation.4 | async-start | bytes 2097152 | tf_op jit(solution)/shard_map/all_to_all | solution.py:828
  183.3 6.6 %copy-start.33 = (f32[32,256]{1,0:T(8,128)S(1)}, f32[32,256]{1,0:T(8,128)}, u32[]{:S(2)}) copy-start(f32[32,256]{1,0:T(8,128)} %constant.106.clone.tc) | copy-start | bytes 98308
  183.3 6.6 %copy-start.37 = (f32[32,256]{1,0:T(8,128)S(1)}, f32[32,256]{1,0:T(8,128)}, u32[]{:S(2)}) copy-start(f32[32,256]{1,0:T(8,128)} %constant.107.clone.ts) | copy-start | bytes 98308
  186.3 21.6 %all-to-all-start.5 = ((f32[32,8,640]{2,1,0:T(8,128)}), f32[32,8,640]{2,1,0:T(8,128)S(1)}, u32[]{:S(2)}, u32[]{:S(2)}) async-start(f32[32,8,640]{2,1,0:T(8,128)} %copy-done.16), calls=%async_computation.5 | async-start | bytes 1310720 | tf_op jit(solution)/shard_map/all_to_all | solution.py:828
  191.0 16.9 %copy-start.15 = (bf16[256,256]{1,0:T(8,128)(2,1)S(1)}, bf16[256,256]{1,0:T(8,128)(2,1)}, u32[]{:S(2)}) copy-start(bf16[256,256]{1,0:T(8,128)(2,1)} %constant.103.clone.ol) | copy-start | bytes 393220
  (38 other events, 43.4 us)

commit v2 on v1

--- a/solution.py
+++ b/solution.py
@@ -7,6 +7,7 @@
 from jax.experimental import pallas as pl
 from jax.experimental.pallas import tpu as pltpu
 from jax.sharding import PartitionSpec as P
+
 
 time_step = 0.25
 highest = lax.Precision.HIGHEST
@@ -124,7 +125,7 @@
     nonlinear_real, nonlinear_imag = spectral(nonlinear, None)
     next_real = (state_real + time_step * (nonlinear_real + forcing[0])) / denominator
     next_imag = (state_imag + time_step * (nonlinear_imag + forcing[1])) / denominator
-    next_field, unused_part = physical(next_real, next_imag, True)
+    next_field, _ = physical(next_real, next_imag, True)
     residual = next_field - target_field
     total = lax.psum(0.5 * jnp.sum(residual * residual), ("px", "py"))
     objective = total / (members * full_first * full_second)
@@ -132,11 +133,11 @@
     coef_real = misfit_real / denominator
     coef_imag = misfit_imag / denominator
     forcing_grad = time_step * jnp.stack([jnp.sum(coef_real, axis=0), jnp.sum(coef_imag, axis=0)])
-    multiplier, unused_other = physical(time_step * coef_real, time_step * coef_imag, True)
+    multiplier, _ = physical(time_step * coef_real, time_step * coef_imag, True)
     joint_real, joint_imag = spectral(multiplier * grad_first, multiplier * grad_second)
     total_real = coef_real - deriv_first * joint_imag + deriv_second * joint_real
     total_imag = coef_imag + deriv_first * joint_real + deriv_second * joint_imag
-    field_grad, unused_last = physical(total_real, total_imag, True)
+    field_grad, _ = physical(total_real, total_imag, True)
     return (next_field, objective, field_grad, forcing_grad)
 
 
@@ -208,16 +209,6 @@
             jnp.asarray(np.sin(angle), jnp.float32),
         )
         half = inner // 2
-        front = np.arange(half)
-        angle = 2.0 * np.pi * (np.outer(front, spot) % inner) / inner
-        real_rows, imag_rows = 2.0 * np.cos(angle), -2.0 * np.sin(angle)
-        real_rows[0] = 1.0
-        imag_rows[0] = np.where(spot % 2 == 0, 1.0, -1.0)
-        self.even_pair = np_split(scale * np.concatenate([real_rows, imag_rows], 0))
-        angle = 2.0 * np.pi * (np.outer(4 + radix * (front + half), spot) % length) / length
-        self.odd_pair = np_split(
-            scale * np.concatenate([2.0 * np.cos(angle), -2.0 * np.sin(angle)], 0)
-        )
         place = np.arange(lanes)
         angle = 2.0 * np.pi * (np.outer(place, place) % lanes) / lanes
         eye = np.eye(inner // lanes)
@@ -355,72 +346,46 @@
         store(one + 4, parts[one][0] - parts[one][1])
 
 
-def rows_inverse(slots, high, low, product, pair, even, odd, spin, store):
+def rows_inverse(slots, high, low, product, pair, spin, store):
     for one in (1, 2, 3):
         put(high, low, one - 1, slots[one])
         put(high, low, 2 + one, slots[4 + one])
     front, back = slice(0, 128), slice(128, 256)
-    put(high, low, 6, jnp.concatenate([slots[0][:, front], slots[4][:, front]], 1))
-    put(high, low, 7, jnp.concatenate([slots[0][:, back], slots[4][:, back]], 1))
-    product[0:384, :] = dots(high[0:384, :], low[0:384, :], pair[0][...], pair[1][...])
-    product[384:448, 0:256] = dots(high[384:448, :], low[384:448, :], even[0][...], even[1][...])
-    product[384:448, 256:512] = dots(high[448:512, :], low[448:512, :], odd[0][...], odd[1][...])
+    real, imag = slots[0], slots[4]
+    first = lax.broadcasted_iota(jnp.int32, (64, 128), 1) == 0
+    none = jnp.zeros((64, 128), jnp.float32)
+    real_front = jnp.where(first, 0.5 * real[:, front], real[:, front])
+    imag_front = jnp.where(first, 0.0, imag[:, front])
+    middle = jnp.where(first, 0.5 * imag[:, front], 0.0)
+    put(high, low, 6, jnp.concatenate([real_front, middle], 1))
+    put(high, low, 7, jnp.concatenate([imag_front, none], 1))
+    put(high, low, 8, jnp.concatenate([none, real[:, back]], 1))
+    put(high, low, 9, jnp.concatenate([none, imag[:, back]], 1))
+    product[0:640, :] = dots(high[0:640, :], low[0:640, :], pair[0][...], pair[1][...])
     for row in range(0, 64, 16):
         for lane in range(0, 256, 128):
-            turned = []
-            for one in (1, 2, 3):
-                at = slice(64 * (one - 1) + row, 64 * (one - 1) + row + 16)
-                to = slice(64 * (2 + one) + row, 64 * (2 + one) + row + 16)
-                lanes, moved = slice(lane, lane + 128), slice(lane + 256, lane + 384)
-                value = (
+            lanes, moved = slice(lane, lane + 128), slice(lane + 256, lane + 384)
+
+            def mixed(real_place, imag_place):
+                at = slice(64 * real_place + row, 64 * real_place + row + 16)
+                to = slice(64 * imag_place + row, 64 * imag_place + row + 16)
+                return (
                     product[at, lanes] - product[to, moved],
                     product[to, lanes] + product[at, moved],
                 )
-                value = turn(
-                    value,
+
+            def spun(one, real_place, imag_place):
+                return turn(
+                    mixed(real_place, imag_place),
                     2.0 * spin[0][one : one + 1, lanes],
                     2.0 * spin[1][one : one + 1, lanes],
                 )
-                turned.append(value)
-            at = slice(384 + row, 400 + row)
+
+            turned = [spun(one, one - 1, 2 + one) for one in (1, 2, 3)]
             eight_inverse(
-                product[at, lane : lane + 128],
-                product[at, lane + 256 : lane + 384],
+                2.0 * mixed(6, 7)[0],
+                spun(4, 8, 9)[0],
                 *turned,
-                lambda one, value: store(one, slice(row, row + 16), slice(lane, lane + 128), value),
-            )
-
-
-def rows_whole(source, offset, high, low, product, pair, spin, store):
-    for place in range(0, 16, 2):
-        both = source[:, :, offset + 64 * place : offset + 64 * place + 128]
-        both = both.reshape(256, 128).T
-        top, bottom = split_of(both)
-        high[64 * place : 64 * place + 128, :] = top
-        low[64 * place : 64 * place + 128, :] = bottom
-    product[...] = dots(high[...], low[...], pair[0][...], pair[1][...])
-    for row in range(0, 64, 16):
-        for lane in range(0, 256, 128):
-            lanes, moved = slice(lane, lane + 128), slice(lane + 256, lane + 384)
-            turned = []
-            for one in range(8):
-                at = slice(64 * one + row, 64 * one + row + 16)
-                to = slice(512 + 64 * one + row, 512 + 64 * one + row + 16)
-                value = (
-                    product[at, lanes] - product[to, moved],
-                    product[to, lanes] + product[at, moved],
-                )
-                turned.append(
-                    turn(value, spin[0][one : one + 1, lanes], spin[1][one : one + 1, lanes])
-                )
-            joint = [
-                (turned[one][0] + turned[8 - one][0], turned[one][1] - turned[8 - one][1])
-                for one in (1, 2, 3)
-            ]
-            eight_inverse(
-                turned[0][0],
-                turned[4][0],
-                *joint,
                 lambda one, value: store(one, slice(row, row + 16), slice(lane, lane + 128), value),
             )
 
@@ -462,8 +427,8 @@
     return tile
 
 
-def cols_inverse(tile, high, low, product, pair, spin, target, offset, count=1):
-    for group in range(count):
+def cols_inverse(tile, high, low, product, pair, spin, targets, offset):
+    for group, target in enumerate(targets):
         for one in range(0, 32, 2):
             first, second = tile(one, group), tile(one + 1, group)
             put_tiles(high, low, one, first[0], second[0], slice(0, 256))
@@ -483,9 +448,9 @@
                 )
             values = butterflies(values, 1)
             for one in range(32):
-                at = offset + 256 * group + lane
+                at = offset + lane
                 target[one, :, at : at + 128] = values[one][0]
-                at += 256 * count
+                at += 256
                 target[one, :, at : at + 128] = values[one][1]
 
 
@@ -507,7 +472,7 @@
     rows_store(slots, out, 0)
 
 
-def kernel_slope(field, ph, pl_, eh, el, oh, ol, sc, ss, deriv, out, high, low, product):
+def kernel_slope(field, ph, pl_, sc, ss, deriv, out, high, low, product):
     def load(one, rows, lanes):
         return field[rows, 256 * one + lanes.start : 256 * one + lanes.stop]
 
@@ -517,11 +482,15 @@
     slots = rows_forward(load, high, low, product, (ph, pl_), (sc, ss), False)
     slots = rows_derived(slots, deriv)
     rows_inverse(
-        slots, high, low, product, (ph, pl_), (eh, el), (oh, ol), (sc, ss), store
-    )
-
-
-def kernel_force(force, ch, cl, tc, ts, out, mixed, turned, spec, high, low, product):
+        slots, high, low, product, (ph, pl_), (sc, ss), store
+    )
+
+
+def kernel_force(
+    place, force, ch, cl, tc, ts,
+    own, far_one, far_two, corner, mixed, back, turned, spec, far, high, low, product,
+):
+    early = place[0] < 16
     for lane in range(0, 2048, 128):
         both = jnp.concatenate([force[part, :, lane : lane + 128] for part in range(2)], 0)
         turned[lane : lane + 128, :] = both.T
@@ -530,14 +499,30 @@
         both = jnp.concatenate(
             [turned[pl.ds(one, 64, stride=32), :], turned[pl.ds(one + 1, 64, stride=32), :]], 0
         ).T
-        base = 64 * one
+        base, base_back = 64 * one, 72 * one
         mixed[base : base + 128, :] = both
         for part in range(2):
-            for kind in range(0, 8, 2):
-                at = base + 64 * part + kind
-                first = mixed[pl.ds(at, 8, stride=8), :]
-                second = mixed[pl.ds(at + 1, 8, stride=8), :]
-                lanes = slice(512 * part + 64 * kind, 512 * part + 64 * kind + 128)
+            start = base_back + 72 * part
+            back[start : start + 8, :] = both[64 * part : 64 * part + 8]
+            for row in range(8):
+                at = start + 64 - 8 * row
+                back[at : at + 8, :] = both[64 * part + 8 * row : 64 * part + 8 * row + 8]
+            at = base + 64 * part
+
+            def rising(kind):
+                return mixed[pl.ds(at + kind, 8, stride=8), :]
+
+            def falling(kind):
+                return back[pl.ds(start + 8 + kind, 8, stride=8), :]
+
+            slots = [jnp.where(early, rising(0), rising(4))]
+            slots += [rising(kind) for kind in (1, 2, 3)]
+            around = back[pl.ds(start, 8, stride=8), :]
+            slots += [jnp.where(early, falling(4), around)]
+            slots += [falling(kind) for kind in (7, 6, 5)]
+            for slot in range(0, 8, 2):
+                first, second = slots[slot], slots[slot + 1]
+                lanes = slice(512 * part + 64 * slot, 512 * part + 64 * slot + 128)
                 spec[8 * one : 8 * one + 8, lanes] = jnp.where(
                     lane < 64, first, pltpu.roll(second, 64, 1)
                 )
@@ -552,42 +537,73 @@
             spec[rows, 512 + 256 * group : 768 + 256 * group],
         )
 
-    cols_inverse(tile, high, low, product, (ch, cl), (tc, ts), out, 0, 2)
-
-
-def kernel_first(source, other, ch, cl, tc, ts, deriv, state, out, high, low, product):
+    cols_inverse(tile, high, low, product, (ch, cl), (tc, ts), [own, far], 0)
+    for one in range(32):
+        corner[one : one + 1, :] = far[one, 0:1, :]
+    far_one[...] = far[0:16]
+    far_two[...] = far[16:32]
+
+
+def kernel_merge(
+    place, own, far_one, far_two, corner, state, ch, cl, tc, ts, out, joint, high, low, product
+):
+    row = lax.broadcasted_iota(jnp.int32, (8, 128), 0)
+    lane = lax.broadcasted_iota(jnp.int32, (8, 128), 1)
+    edge = jnp.logical_and(row == 0, lane < 64)
+    fixed = jnp.logical_and(edge, place[0] < 16)
+    packed = jnp.logical_and(edge, place[0] == 0)
+    for one in range(32):
+        far, at = (far_one, one) if one < 16 else (far_two, one - 16)
+        for start in range(0, 256, 128):
+            lanes, moved = slice(start, start + 128), slice(start + 256, start + 384)
+            own_real, own_imag = own[one, :, lanes], own[one, :, moved]
+            far_real, far_imag = far[at, :, lanes], far[at, :, moved]
+            if start == 0:
+                far_real = jnp.where(fixed, corner[one : one + 1, lanes], far_real)
+                far_imag = jnp.where(fixed, corner[one : one + 1, moved], far_imag)
+            real, imag = 0.5 * (own_real + far_real), 0.5 * (own_imag - far_imag)
+            if start == 0:
+                real = jnp.where(packed, own_real, real)
+                imag = jnp.where(packed, far_real, imag)
+            joint[one, :, lanes] = real
+            joint[one, :, moved] = imag
+    tile = cols_forward(joint, 0, high, low, product, (ch, cl), (tc, ts))
+    for one in range(32):
+        rows = slice(8 * one, 8 * one + 8)
+        real, imag = tile(one)
+        out[0, rows, :] = state[0, rows, :] + time_step * real
+        out[1, rows, :] = state[1, rows, :] + time_step * imag
+
+
+def kernel_first(source, ahead, ch, cl, tc, ts, deriv, state, out, high, low, product):
     tile = cols_forward(source, 0, high, low, product, (ch, cl), (tc, ts))
     for one in range(32):
         rows = slice(8 * one, 8 * one + 8)
         real, imag = tile(one)
         state[0, rows, :] = real
         state[1, rows, :] = imag
+    state.send()
 
     def slope(one, group):
         rows = slice(8 * one, 8 * one + 8)
         wave = deriv[one : one + 1, :]
         return -wave * state[1, rows, :], wave * state[0, rows, :]
 
-    cols_inverse(slope, high, low, product, (ch, cl), (tc, ts), out, 0)
-    out[:, :, 512:1536] = other[...]
+    cols_inverse(slope, high, low, product, (ch, cl), (tc, ts), [out], 0)
 
 
 def kernel_bend(
-    source, second, other, ph, pl_, eh, el, oh, ol, sc, ss, grad, out, bend, high, low, product
+    source, second, other, ph, pl_, sc, ss, grad, out, bend, high, low, product
 ):
-    def put_bend(one, rows, lanes, value):
-        bend[rows, 256 * one + lanes.start : 256 * one + lanes.stop] = value
-
-    rows_whole(source, 512, high, low, product, (ph, pl_), (sc, ss), put_bend)
-
     def store(one, rows, lanes, value):
         to = slice(256 * one + lanes.start, 256 * one + lanes.stop)
         grad[rows, to] = value
         side = second[rows, to]
-        bend[rows, to] = bend[rows, to] - 0.5 * (value * value + side * side)
+        bend[rows, to] = -0.5 * (value * value + side * side)
 
     slots = rows_loaded(source, 0)
-    rows_inverse(slots, high, low, product, (ph, pl_), (eh, el), (oh, ol), (sc, ss), store)
+    rows_inverse(slots, high, low, product, (ph, pl_), (sc, ss), store)
+    grad.send()
 
     def load(one, rows, lanes):
         return bend[rows, 256 * one + lanes.start : 256 * one + lanes.stop]
@@ -632,7 +648,6 @@
             for part in range(2)
         )
 
-    held = []
     for one in range(32):
         rows = slice(8 * one, 8 * one + 8)
         value = (fresh[0, rows, :], fresh[1, rows, :])
@@ -650,6 +665,7 @@
             coef[part, rows, :] = time_step * slope[part]
             goal_next = following[part]
             product[256 * part + 8 * one : 256 * part + 8 * one + 8, 0:256] = goal_next
+    coef.send()
     for part in range(2):
         fresh[part, :, :] = product[256 * part : 256 * part + 256, 0:256]
 
@@ -661,12 +677,12 @@
         rows = slice(8 * one, 8 * one + 8)
         return fresh[0, rows, :], fresh[1, rows, :]
 
-    cols_inverse(scaled, high, low, product, (ch, cl), (tc, ts), out, 0)
-    cols_inverse(following_tile, high, low, product, (ch, cl), (tc, ts), out, 512)
+    cols_inverse(scaled, high, low, product, (ch, cl), (tc, ts), [out], 0)
+    cols_inverse(following_tile, high, low, product, (ch, cl), (tc, ts), [out], 512)
 
 
 def kernel_adjoint(
-    source, grad, ph, pl_, eh, el, oh, ol, sc, ss, mult, out, joint, high, low, product
+    source, grad, ph, pl_, sc, ss, mult, out, joint, high, low, product
 ):
     def store(one, rows, lanes, value):
         to = slice(256 * one + lanes.start, 256 * one + lanes.stop)
@@ -674,7 +690,8 @@
         joint[rows, to] = value * grad[rows, to]
 
     slots = rows_loaded(source, 0)
-    rows_inverse(slots, high, low, product, (ph, pl_), (eh, el), (oh, ol), (sc, ss), store)
+    rows_inverse(slots, high, low, product, (ph, pl_), (sc, ss), store)
+    mult.send()
 
     def load(one, rows, lanes):
         return joint[rows, 256 * one + lanes.start : 256 * one + lanes.stop]
@@ -690,7 +707,7 @@
 
 
 def kernel_side(
-    source, goal, mult, second, ph, pl_, eh, el, oh, ol, sc, ss, deriv,
+    source, goal, mult, second, ph, pl_, sc, ss, deriv,
     ahead, side, miss, joint, high, low, product,
 ):
     def store(one, rows, lanes, value):
@@ -699,7 +716,7 @@
         joint[rows, to] = mult[rows, to] * second[rows, to]
 
     slots = rows_loaded(source, 512)
-    rows_inverse(slots, high, low, product, (ph, pl_), (eh, el), (oh, ol), (sc, ss), store)
+    rows_inverse(slots, high, low, product, (ph, pl_), (sc, ss), store)
     total = jnp.zeros((8, 256), jnp.float32)
     for row in range(0, 64, 8):
         for lane in range(0, 2048, 256):
@@ -729,7 +746,7 @@
         rows = slice(8 * one, 8 * one + 8)
         return spec[0, rows, :], spec[1, rows, :]
 
-    cols_inverse(whole, high, low, product, (ch, cl), (tc, ts), out, 0)
+    cols_inverse(whole, high, low, product, (ch, cl), (tc, ts), [out], 0)
     out[:, :, 512:640] = jnp.broadcast_to(miss[...][None], (32, 8, 128))
 
 
@@ -791,29 +808,80 @@
             out[part, :, start : start + 128] = both[64 * part : 64 * part + 64]
 
 
-def kernel_finish(source, side, ph, pl_, eh, el, oh, ol, sc, ss, out, total, high, low, product):
+def kernel_finish(source, side, ph, pl_, sc, ss, out, total, high, low, product):
     slots = rows_loaded(source, 0)
     slots = [slots[place] + side[64 * place : 64 * place + 64, :] for place in range(8)]
 
     def store(one, rows, lanes, value):
         out[rows, 256 * one + lanes.start : 256 * one + lanes.stop] = value
 
-    rows_inverse(slots, high, low, product, (ph, pl_), (eh, el), (oh, ol), (sc, ss), store)
-    total[...] = jnp.sum(source[:, :, 512:640], axis=0)
-
-
-def call(body, outputs, scratch, *operands, scalars=0):
+    rows_inverse(slots, high, low, product, (ph, pl_), (sc, ss), store)
+    total[0, 0] = jnp.sum(source[:, 0:1, 512:640]) * (1.0 / (128.0 * out.formed.shape[1] ** 2))
+
+
+class Leaving:
+    def __init__(self, formed, copy):
+        self.formed, self.copy, self.gone = formed, copy, False
+
+    def send(self):
+        if not self.gone:
+            self.copy.start()
+            self.gone = True
+
+    def __getitem__(self, index):
+        return self.formed[index]
+
+    def __setitem__(self, index, value):
+        self.formed[index] = value
+
+
+def call(body, outputs, scratch, *operands, scalars=0, near=0, number=False):
+    lead_count = scalars + near
+    fields = operands[lead_count:]
+    count, made = len(fields), len(outputs)
+
+    def whole(*refs):
+        lead, refs = refs[:lead_count], refs[lead_count:]
+        given, results, refs = refs[:count], refs[count : count + made], refs[count + made :]
+        last, refs = (refs[:1], refs[1:]) if number else ((), refs)
+        held, formed, refs = refs[:count], refs[count : count + made], refs[count + made :]
+        extra, into, onto = refs[:-2], refs[-2], refs[-1]
+        arrivals = [
+            pltpu.make_async_copy(given[one], held[one], into.at[one]) for one in range(count)
+        ]
+        for one in arrivals:
+            one.start()
+        departures = [
+            Leaving(formed[one], pltpu.make_async_copy(formed[one], results[one], onto.at[one]))
+            for one in range(made)
+        ]
+        for one in arrivals:
+            one.wait()
+        body(*lead, *held, *departures, *last, *extra)
+        for one in departures:
+            one.send()
+        for one in departures:
+            one.copy.wait()
+
     specs = [pl.BlockSpec(memory_space=pltpu.SMEM)] * scalars
-    specs += [pl.BlockSpec(memory_space=pltpu.VMEM)] * (len(operands) - scalars)
+    specs += [pl.BlockSpec(memory_space=pltpu.VMEM)] * near
+    specs += [pl.BlockSpec(memory_space=pltpu.HBM)] * count
+    scratch = (
+        [pltpu.VMEM(one.shape, one.dtype) for one in fields]
+        + [pltpu.VMEM(one, jnp.float32) for one in outputs]
+        + scratch
+        + [pltpu.SemaphoreType.DMA((count,)), pltpu.SemaphoreType.DMA((made,))]
+    )
     return pl.pallas_call(
-        body,
-        out_shape=tuple(jax.ShapeDtypeStruct(one, jnp.float32) for one in outputs),
+        whole,
+        out_shape=tuple(pltpu.HBM(one, jnp.float32) for one in outputs)
+        + (jax.ShapeDtypeStruct((1, 1), jnp.float32),) * number,
         in_specs=specs,
-        out_specs=tuple(pl.BlockSpec(memory_space=pltpu.VMEM) for _ in outputs),
+        out_specs=tuple(pl.BlockSpec(memory_space=pltpu.HBM) for _ in outputs)
+        + (pl.BlockSpec(memory_space=pltpu.SMEM),) * number,
         scratch_shapes=scratch,
-        name=body.__name__,
-        compiler_params=pltpu.CompilerParams(vmem_limit_bytes=48 * 2**20),
-    )(*operands)
+        compiler_params=pltpu.CompilerParams(vmem_limit_bytes=24 * 2**20),
+    )(*operands[:lead_count], *[pltpu.with_memory_space_constraint(one, pltpu.HBM) for one in fields])
 
 
 def work(rows):
@@ -836,8 +904,7 @@
     tables = Tables(length, parts)
     inner = length // 8
     field, goal = initial_field[0], target_field[0]
-    rows_all = tables.row_pair + tables.even_pair + tables.odd_pair + tables.row_turn
-    rows_some = tables.row_pair + tables.row_turn
+    rows = tables.row_pair + tables.row_turn
     cols = tables.col_pair + tables.col_turn
     f32 = jnp.float32
     own = jnp.arange(8, dtype=jnp.int32)[None, :, None]
@@ -858,40 +925,72 @@
     cross = jnp.where(packed, 0.5 * (plain - middle), 0.0).reshape(inner, inner)[:, :128]
 
     block = (parts, 8, 512)
-    (sent,) = call(kernel_start, [block], work(576), field, *rows_some)
+    (sent,) = call(kernel_start, [block], work(640), field, *rows)
     first = exchange(sent)
-    (force,) = call(
+    spot = jnp.asarray(device, jnp.int32).reshape(1)
+    half_block = (parts // 2, 8, 512)
+    own_force, far_one, far_two, corner_own = call(
         kernel_force,
-        [(parts, 8, 1024)],
-        [pltpu.VMEM((length, 128), f32), pltpu.VMEM((length, 128), f32), pltpu.VMEM((256, 1024), f32)]
+        [block, half_block, half_block, (parts, 512)],
+        [
+            pltpu.VMEM((length, 128), f32),
+            pltpu.VMEM((length + 256, 128), f32),
+            pltpu.VMEM((length, 128), f32),
+            pltpu.VMEM((256, 1024), f32),
+            pltpu.VMEM(block, f32),
+        ]
         + work(512),
+        spot,
         forcing,
         *cols,
-    )
-    (goal_rows,) = call(kernel_start, [block], work(576), goal, *rows_some)
+        scalars=1,
+    )
+    middle_part = parts // 2
+    mirror = [(one, parts - 1 - one) for one in range(parts)]
+    around = [(middle_part, 0)]
+    around += [(middle_part + one, middle_part - one) for one in range(1, middle_part)]
+    far_one = lax.ppermute(far_one, ("px", "py"), mirror)
+    far_two = lax.ppermute(far_two, ("px", "py"), mirror)
+    corner = lax.ppermute(corner_own, ("px", "py"), around)
+    (goal_rows,) = call(kernel_start, [block], work(640), goal, *rows)
     (grad_second,) = call(
-        kernel_slope, [(local, length)], work(576), field, *rows_all, tables.row_deriv
+        kernel_slope, [(local, length)], work(640), field, *rows, tables.row_deriv
     )
     state, sent = call(
         kernel_first,
-        [(2, 256, 256), (parts, 8, 1536)],
+        [(2, 256, 256), block],
         work(512),
         first,
-        force,
+        corner_own,
         *cols,
         tables.col_deriv,
+        near=1,
     )
     moved = exchange(sent)
     grad_first, sent = call(
         kernel_bend,
         [(local, length), (parts, 8, 1024)],
-        [pltpu.VMEM((local, length), f32)] + work(1024),
+        [pltpu.VMEM((local, length), f32)] + work(640),
         moved,
         grad_second,
         goal_rows,
-        *rows_all,
+        *rows,
+        near=1,
     )
     moved = exchange(sent)
+    (state,) = call(
+        kernel_merge,
+        [(2, 256, 256)],
+        [pltpu.VMEM(block, f32)] + work(512),
+        spot,
+        own_force,
+        far_one,
+        far_two,
+        corner,
+        state,
+        *cols,
+        scalars=1,
+    )
     coef, sent = call(
         kernel_solve,
         [(2, 256, 256), (parts, 8, 1024)],
@@ -901,25 +1000,27 @@
         damp,
         cross,
         *cols,
+        near=1,
     )
     moved = exchange(sent)
     mult, sent = call(
         kernel_adjoint,
         [(local, length), (parts, 8, 1024)],
-        [pltpu.VMEM((local, length), f32)] + work(576),
+        [pltpu.VMEM((local, length), f32)] + work(640),
         moved,
         grad_first,
-        *rows_all,
+        *rows,
+        near=1,
     )
     next_field, side, miss = call(
         kernel_side,
         [(local, length), (512, 256), (8, 128)],
-        [pltpu.VMEM((local, length), f32)] + work(576),
+        [pltpu.VMEM((local, length), f32)] + work(640),
         moved,
         goal,
         mult,
         grad_second,
-        *rows_all,
+        *rows,
         tables.row_deriv,
     )
     moved = exchange(sent)
@@ -932,12 +1033,13 @@
         miss,
         *cols,
         tables.col_deriv,
+        near=1,
     )
     (forcing_grad,) = call(
         kernel_force_grad,
         [(2, local, length)],
         [pltpu.VMEM((length, 128), f32), pltpu.VMEM((length, 128), f32)] + work(512),
-        jnp.asarray(device, jnp.int32).reshape(1),
+        spot,
         moved,
         coef,
         *cols,
@@ -945,9 +1047,9 @@
     )
     moved = exchange(sent)
     field_grad, total = call(
-        kernel_finish, [(local, length), (8, 128)], work(576), moved, side, *rows_all
-    )
-    objective = total[0, 0] / (length * length)
+        kernel_finish, [(local, length)], work(640), moved, side, *rows, near=1, number=True
+    )
+    objective = total.reshape(())
     return (next_field[None], objective, field_grad[None], forcing_grad)
 
 

time: 214 us -> 213 us (level)
  Pallas kernels: 26.8 us -> 55.6 us
  local copies, waits for them, and re-layouts: 27.1 us -> 0.86 us
  waiting for transfers between devices: 105 us -> 85.8 us
  blocking collectives: 29.6 us -> 39 us
  starting transfers between devices: 21.5 us -> 28.2 us
    all_to_all x5, waiting for transfers between devices: 105 us -> 54.2 us  [exchange(): lax.all_to_all(value, ('px', 'py'), split_axis=0, concat_axis=0, tiled=True)]
    ppermute x0 -> x3, waiting for transfers between devices: none -> 31.6 us  [the longest x1 31.6 us: per_device_fast(): corner = lax.ppermute(corner_own, ('px', 'py'), around)]
    pallas_call x12 -> x13, Pallas kernels: 26.8 us -> 55.6 us  [call(): pl.pallas_call(whole, out_shape=tuple((pltpu.HBM(one, jnp.float32) for on...]
    unnamed x114 -> x18, local copies, waits for them, and re-layouts: 26.5 us -> 0.84 us
    all_to_all x1, blocking collectives: 29.6 us -> 39 us  [exchange(): lax.all_to_all(value, ('px', 'py'), split_axis=0, concat_axis=0, tiled=True)]
    ppermute x0 -> x3, starting transfers between devices: none -> 7.44 us  [the longest x1 5.88 us: per_device_fast(): far_one = lax.ppermute(far_one, ('px', 'py'), mirror)]
  transfers between devices with their start and end apart: 5 -> 8, of which waited for: 5 -> 5; matrix products, arithmetic and copies ran while one was open for 0% -> 1% of each run, Pallas kernels for 5% -> 11%
where the time goes in v2:
time: 213 us; the launch traced here: 212 us
  waiting for transfers between devices  85.8 us (40%)
  Pallas kernels  55.6 us (26%)
  blocking collectives  39 us (18%)
  starting transfers between devices  28.2 us (13%)
    pallas_call x13, Pallas kernels, call(): pl.pallas_call(whole, out_shape=tuple((pltpu.HBM(one, jnp.float32) for on...  55.6 us
    all_to_all x5, waiting for transfers between devices, exchange(): lax.all_to_all(value, ('px', 'py'), split_axis=0, concat_axis=0, tiled=True)  54.2 us
    all_to_all x1, blocking collectives, exchange(): lax.all_to_all(value, ('px', 'py'), split_axis=0, concat_axis=0, tiled=True)  39 us
    ppermute x1, waiting for transfers between devices, per_device_fast(): corner = lax.ppermute(corner_own, ('px', 'py'), around)  31.6 us
    all_to_all x5, starting transfers between devices, exchange(): lax.all_to_all(value, ('px', 'py'), split_axis=0, concat_axis=0, tiled=True)  20.8 us
    ppermute x1, starting transfers between devices, per_device_fast(): far_one = lax.ppermute(far_one, ('px', 'py'), mirror)  5.88 us
  transfers between devices with their start and end apart: 8, of which 5 were waited for; matrix products, arithmetic and copies ran while one was open for 1% of the time, Pallas kernels for 11%

profile of v2, /device:TPU:0, one launch (start us, length us, event | category | flops | bytes accessed | tf_op | source)
XLA Modules:
  0.0 212.1 jit_solution(12270421061952317852)
XLA Ops:
  3.6 7.3 %all-to-all-start = ((f32[32,8,512]{2,1,0:T(8,128)}), f32[32,8,512]{2,1,0:T(8,128)S(1)}, u32[]{:S(2)}, u32[]{:S(2)}) async-start(f32[32,8,512]{2,1,0:T(8,128)} %shard_map.165), calls=%async_computation | async-start | bytes 1048576 | tf_op jit(solution)/shard_map/all_to_all | solution.py:896
  10.9 4.9 %shard_map.166 = (f32[32,8,512]{2,1,0:T(8,128)}, f32[16,8,512]{2,1,0:T(8,128)}, f32[16,8,512]{2,1,0:T(8,128)}, f32[32,512]{1,0:T(8,128)}) custom-call(s32[1]{0:T(128)} %bitcast.1.refs_0_, f32[2,64,2048]{2,1,0:T(8,128)} %refs_1_.4, bf16[256,512]{1,0:T(8,128)(2,1)} %constant.88.clone.refs_2_.refs_6_.refs_4_.refs_3_, ...), custom_call_target="tpu_custom_call" | custom-call | tf_op jit(solution)/shard_map/pallas_call | solution.py:875
  15.8 10.7 %all-to-all-done.refs_0_ = f32[32,8,512]{2,1,0:T(8,128)S(1)} async-done(((f32[32,8,512]{2,1,0:T(8,128)}), f32[32,8,512]{2,1,0:T(8,128)S(1)}, u32[]{:S(2)}, u32[]{:S(2)}) %all-to-all-start) | async-done | bytes 524320 | tf_op jit(solution)/shard_map/all_to_all | solution.py:896
  26.5 4.0 %shard_map.167 = (f32[2,256,256]{2,1,0:T(8,128)}, f32[32,8,512]{2,1,0:T(8,128)}) custom-call(f32[32,8,512]{2,1,0:T(8,128)S(1)} %all-to-all-done.refs_0_, f32[32,512]{1,0:T(8,128)} %get-tuple-element.21.refs_1_, bf16[256,512]{1,0:T(8,128)(2,1)} %constant.88.clone.refs_2_.refs_6_.refs_4_.refs_3_, ...), custom_call_target="tpu_custom_call" | custom-call | tf_op jit(solution)/shard_map/pallas_call | solution.py:875
  30.6 3.0 %all-to-all-start.1 = ((f32[32,8,512]{2,1,0:T(8,128)}), f32[32,8,512]{2,1,0:T(8,128)S(1)}, u32[]{:S(2)}, u32[]{:S(2)}) async-start(f32[32,8,512]{2,1,0:T(8,128)} %get-tuple-element.22), calls=%async_computation.1 | async-start | bytes 1048576 | tf_op jit(solution)/shard_map/all_to_all | solution.py:896
  33.5 4.2 %shard_map.168.refs_1_.refs_3_ = f32[64,2048]{1,0:T(8,128)} custom-call(f32[64,2048]{1,0:T(8,128)} %bitcast.18, bf16[256,512]{1,0:T(8,128)(2,1)} %constant.84.clone.refs_1_.refs_3_.refs_2_.refs_4_, bf16[256,512]{1,0:T(8,128)(2,1)} %constant.85.clone.refs_2_.refs_4_.refs_3_.refs_5_, f32[8,256]{1,0:T(8,128)} %constant.86.clone.refs_3_.refs_5_.refs_4_.refs_6_, ...), custom_call_target="tpu_custom_call" | custom-call | tf_op jit(solution)/shard_map/pallas_call | solution.py:875
  37.8 3.0 %shard_map.169.refs_2_ = f32[32,8,512]{2,1,0:T(8,128)} custom-call(f32[64,2048]{1,0:T(8,128)} %bitcast.19, bf16[256,512]{1,0:T(8,128)(2,1)} %constant.84.clone.refs_1_.refs_3_.refs_2_.refs_4_, bf16[256,512]{1,0:T(8,128)(2,1)} %constant.85.clone.refs_2_.refs_4_.refs_3_.refs_5_, f32[8,256]{1,0:T(8,128)} %constant.86.clone.refs_3_.refs_5_.refs_4_.refs_6_, ...), custom_call_target="tpu_custom_call" | custom-call | tf_op jit(solution)/shard_map/pallas_call | solution.py:875
  40.7 8.4 %all-to-all-done.1.refs_0_ = f32[32,8,512]{2,1,0:T(8,128)S(1)} async-done(((f32[32,8,512]{2,1,0:T(8,128)}), f32[32,8,512]{2,1,0:T(8,128)S(1)}, u32[]{:S(2)}, u32[]{:S(2)}) %all-to-all-start.1) | async-done | bytes 524320 | tf_op jit(solution)/shard_map/all_to_all | solution.py:896
  49.2 5.0 %shard_map.170 = (f32[64,2048]{1,0:T(8,128)}, f32[32,8,1024]{2,1,0:T(8,128)}) custom-call(f32[32,8,512]{2,1,0:T(8,128)S(1)} %all-to-all-done.1.refs_0_, f32[64,2048]{1,0:T(8,128)} %shard_map.168.refs_1_.refs_3_, f32[32,8,512]{2,1,0:T(8,128)} %shard_map.169.refs_2_, bf16[256,512]{1,0:T(8,128)(2,1)} %constant.84.clone.refs_1_.refs_3_.refs_2_.refs_4_, ...), custom_call_target="tpu_custom_call" | custom-call | tf_op jit(solution)/shard_map/pallas_call | solution.py:875
  54.2 3.0 %all-to-all-start.2 = ((f32[32,8,1024]{2,1,0:T(8,128)}), f32[32,8,1024]{2,1,0:T(8,128)S(1)}, u32[]{:S(2)}, u32[]{:S(2)}) async-start(f32[32,8,1024]{2,1,0:T(8,128)} %get-tuple-element.23), calls=%async_computation.2 | async-start | bytes 2097152 | tf_op jit(solution)/shard_map/all_to_all | solution.py:896
  58.7 5.9 %collective-permute-start = (f32[16,8,512]{2,1,0:T(8,128)S(1)}, f32[16,8,512]{2,1,0:T(8,128)S(1)}, u32[]{:S(2)}, u32[]{:S(2)}) collective-permute-start(f32[16,8,512]{2,1,0:T(8,128)S(1)} %copy-done.8), channel_id=1, source_target_pairs={{0,31},{1,30},{2,29},{3,28},{4,27},{5,26},{6,25},{7,24},{8,23},{9,... | collective-permute-start | bytes 786440 | tf_op jit(solution)/shard_map/ppermute | solution.py:952
  66.4 31.6 %collective-permute-done.2.refs_4_ = f32[32,512]{1,0:T(8,128)S(1)} collective-permute-done((f32[32,512]{1,0:T(8,128)S(1)}, f32[32,512]{1,0:T(8,128)S(1)}, u32[]{:S(2)}, u32[]{:S(2)}) %collective-permute-start.2) | collective-permute-done | bytes 65568 | tf_op jit(solution)/shard_map/ppermute | solution.py:954
  98.9 3.3 %shard_map.171.refs_1_ = f32[2,256,256]{2,1,0:T(8,128)} custom-call(s32[1]{0:T(128)} %bitcast.1.refs_0_, f32[32,8,512]{2,1,0:T(8,128)} %get-tuple-element.24.refs_1_, f32[16,8,512]{2,1,0:T(8,128)} %copy-done.2, f32[16,8,512]{2,1,0:T(8,128)} %copy-done.3, f32[32,512]{1,0:T(8,128)} %copy-done.5, f32[2,256,256]{2,1,0:T(8,128)} %get-tuple-element.27.refs_5_, ...), custom_call_target="tpu_custom_call" | custom-call | tf_op jit(solution)/shard_map/pallas_call | solution.py:875
  102.2 5.3 %shard_map.172 = (f32[2,256,256]{2,1,0:T(8,128)}, f32[32,8,1024]{2,1,0:T(8,128)}) custom-call(f32[32,8,1024]{2,1,0:T(8,128)S(1)} %all-to-all-done.2.refs_0_, f32[2,256,256]{2,1,0:T(8,128)} %shard_map.171.refs_1_, f32[256,256]{1,0:T(8,128)} %get-tuple-element.39.refs_2_, f32[256,128]{1,0:T(8,128)} %fusion.7.refs_3_, ...), custom_call_target="tpu_custom_call" | custom-call | tf_op jit(solution)/shard_map/pallas_call | solution.py:875
  107.5 39.0 %all_to_all.30.refs_0_ = f32[32,8,1024]{2,1,0:T(8,128)S(1)} all-to-all(f32[32,8,1024]{2,1,0:T(8,128)} %get-tuple-element.28), channel_id=1, replica_groups=mesh['px'=8,'py'=4] {'px','py'}, dimensions={0} | all-to-all | bytes 2097152 | tf_op jit(solution)/shard_map/all_to_all | solution.py:896
  146.5 6.0 %shard_map.173 = (f32[64,2048]{1,0:T(8,128)}, f32[32,8,1024]{2,1,0:T(8,128)}) custom-call(f32[32,8,1024]{2,1,0:T(8,128)S(1)} %all_to_all.30.refs_0_, f32[64,2048]{1,0:T(8,128)} %get-tuple-element.29.refs_1_, bf16[256,512]{1,0:T(8,128)(2,1)} %constant.84.clone.refs_1_.refs_3_.refs_2_.refs_4_, bf16[256,512]{1,0:T(8,128)(2,1)} %constant.85.clone.refs_2_.refs_4_.refs_3_.refs_5_, ...), custom_call_target="tpu_custom_call" | custom-call | tf_op jit(solution)/shard_map/pallas_call | solution.py:875
  152.5 3.6 %all-to-all-start.4 = ((f32[32,8,1024]{2,1,0:T(8,128)}), f32[32,8,1024]{2,1,0:T(8,128)S(1)}, u32[]{:S(2)}, u32[]{:S(2)}) async-start(f32[32,8,1024]{2,1,0:T(8,128)} %get-tuple-element.32), calls=%async_computation.4 | async-start | bytes 2097152 | tf_op jit(solution)/shard_map/all_to_all | solution.py:896
  156.1 4.3 %shard_map.174 = (f32[64,2048]{1,0:T(8,128)}, f32[512,256]{1,0:T(8,128)}, f32[8,128]{1,0:T(8,128)}) custom-call(f32[32,8,1024]{2,1,0:T(8,128)} %copy-done.1, f32[64,2048]{1,0:T(8,128)} %bitcast.20, f32[64,2048]{1,0:T(8,128)} %get-tuple-element.30.refs_2_, f32[64,2048]{1,0:T(8,128)} %shard_map.168.refs_1_.refs_3_, ...), custom_call_target="tpu_custom_call" | custom-call | tf_op jit(solution)/shard_map/pallas_call | solution.py:875
  160.4 21.9 %all-to-all-done.4.refs_0_.refs_1_ = f32[32,8,1024]{2,1,0:T(8,128)S(1)} async-done(((f32[32,8,1024]{2,1,0:T(8,128)}), f32[32,8,1024]{2,1,0:T(8,128)S(1)}, u32[]{:S(2)}, u32[]{:S(2)}) %all-to-all-start.4) | async-done | bytes 1048608 | tf_op jit(solution)/shard_map/all_to_all | solution.py:896
  182.3 4.6 %shard_map.175 = f32[32,8,640]{2,1,0:T(8,128)} custom-call(f32[32,8,1024]{2,1,0:T(8,128)S(1)} %all-to-all-done.4.refs_0_.refs_1_, f32[2,256,256]{2,1,0:T(8,128)} %get-tuple-element.33.refs_1_.refs_2_, f32[8,128]{1,0:T(8,128)} %get-tuple-element.34.refs_2_, bf16[256,512]{1,0:T(8,128)(2,1)} %constant.88.clone.refs_2_.refs_6_.refs_4_.refs_3_, ...), custom_call_target="tpu_custom_call" | custom-call | tf_op jit(solution)/shard_map/pallas_call | solution.py:875
  187.0 3.8 %all-to-all-start.5 = ((f32[32,8,640]{2,1,0:T(8,128)}), f32[32,8,640]{2,1,0:T(8,128)S(1)}, u32[]{:S(2)}, u32[]{:S(2)}) async-start(f32[32,8,640]{2,1,0:T(8,128)} %shard_map.175), calls=%async_computation.5 | async-start | bytes 1310720 | tf_op jit(solution)/shard_map/all_to_all | solution.py:896
  190.8 4.6 %shard_map.177 = f32[2,64,2048]{2,1,0:T(8,128)} custom-call(s32[1]{0:T(128)} %bitcast.1.refs_0_, f32[32,8,1024]{2,1,0:T(8,128)} %copy-done, f32[2,256,256]{2,1,0:T(8,128)} %get-tuple-element.33.refs_1_.refs_2_, bf16[256,512]{1,0:T(8,128)(2,1)} %constant.88.clone.refs_2_.refs_6_.refs_4_.refs_3_, ...), custom_call_target="tpu_custom_call" | custom-call | tf_op jit(solution)/shard_map/pallas_call | solution.py:875
  195.5 13.1 %all-to-all-done.5.refs_0_ = f32[32,8,640]{2,1,0:T(8,128)S(1)} async-done(((f32[32,8,640]{2,1,0:T(8,128)}), f32[32,8,640]{2,1,0:T(8,128)S(1)}, u32[]{:S(2)}, u32[]{:S(2)}) %all-to-all-start.5) | async-done | bytes 655392 | tf_op jit(solution)/shard_map/all_to_all | solution.py:896
  208.6 3.4 %shard_map.176 = (f32[64,2048]{1,0:T(8,128)}, f32[1,1]{1,0:T(1,128)}) custom-call(f32[32,8,640]{2,1,0:T(8,128)S(1)} %all-to-all-done.5.refs_0_, f32[512,256]{1,0:T(8,128)} %get-tuple-element.35.refs_1_, bf16[256,512]{1,0:T(8,128)(2,1)} %constant.84.clone.refs_1_.refs_3_.refs_2_.refs_4_, bf16[256,512]{1,0:T(8,128)(2,1)} %constant.85.clone.refs_2_.refs_4_.refs_3_.refs_5_, ...), custom_call_target="tpu_custom_call" | custom-call | tf_op jit(solution)/shard_map/pallas_call | solution.py:875
  (32 shorter events, 7.0 us)
Async XLA Ops:
  3.6 23.0 %all-to-all-start = ((f32[32,8,512]{2,1,0:T(8,128)}), f32[32,8,512]{2,1,0:T(8,128)S(1)}, u32[]{:S(2)}, u32[]{:S(2)}) async-start(f32[32,8,512]{2,1,0:T(8,128)} %shard_map.165), calls=%async_computation | async-start | bytes 1048576 | tf_op jit(solution)/shard_map/all_to_all | solution.py:896
  30.6 18.6 %all-to-all-start.1 = ((f32[32,8,512]{2,1,0:T(8,128)}), f32[32,8,512]{2,1,0:T(8,128)S(1)}, u32[]{:S(2)}, u32[]{:S(2)}) async-start(f32[32,8,512]{2,1,0:T(8,128)} %get-tuple-element.22), calls=%async_computation.1 | async-start | bytes 1048576 | tf_op jit(solution)/shard_map/all_to_all | solution.py:896
  54.2 3.0 %copy-start.4 = (f32[32,512]{1,0:T(8,128)S(1)}, f32[32,512]{1,0:T(8,128)}, u32[]{:S(2)}) copy-start(f32[32,512]{1,0:T(8,128)} %get-tuple-element.21.refs_1_) | copy-start | bytes 196612
  54.2 4.5 %copy-start.8 = (f32[16,8,512]{2,1,0:T(8,128)S(1)}, f32[16,8,512]{2,1,0:T(8,128)}, u32[]{:S(2)}) copy-start(f32[16,8,512]{2,1,0:T(8,128)} %get-tuple-element.25) | copy-start | bytes 786436
  54.2 10.4 %copy-start.7 = (f32[16,8,512]{2,1,0:T(8,128)S(1)}, f32[16,8,512]{2,1,0:T(8,128)}, u32[]{:S(2)}) copy-start(f32[16,8,512]{2,1,0:T(8,128)} %get-tuple-element.26) | copy-start | bytes 786436
  54.2 48.0 %all-to-all-start.2 = ((f32[32,8,1024]{2,1,0:T(8,128)}), f32[32,8,1024]{2,1,0:T(8,128)S(1)}, u32[]{:S(2)}, u32[]{:S(2)}) async-start(f32[32,8,1024]{2,1,0:T(8,128)} %get-tuple-element.23), calls=%async_computation.2 | async-start | bytes 2097152 | tf_op jit(solution)/shard_map/all_to_all | solution.py:896
  57.2 7.7 %copy-start.6 = (f32[32,256]{1,0:T(8,128)S(1)}, f32[32,256]{1,0:T(8,128)}, u32[]{:S(2)}) copy-start(f32[32,256]{1,0:T(8,128)} %constant.95) | copy-start | bytes 98308
  57.2 40.8 %collective-permute-start.2 = (f32[32,512]{1,0:T(8,128)S(1)}, f32[32,512]{1,0:T(8,128)S(1)}, u32[]{:S(2)}, u32[]{:S(2)}) collective-permute-start(f32[32,512]{1,0:T(8,128)S(1)} %copy-done.4), channel_id=1, source_target_pairs={{16,0},{17,15},{18,14},{19,13},{20,12},{21,11},{22,10},{23,9},{24,... | collective-permute-start | bytes 196616 | tf_op jit(solution)/shard_map/ppermute | solution.py:954
  58.7 39.3 %collective-permute-start = (f32[16,8,512]{2,1,0:T(8,128)S(1)}, f32[16,8,512]{2,1,0:T(8,128)S(1)}, u32[]{:S(2)}, u32[]{:S(2)}) collective-permute-start(f32[16,8,512]{2,1,0:T(8,128)S(1)} %copy-done.8), channel_id=1, source_target_pairs={{0,31},{1,30},{2,29},{3,28},{4,27},{5,26},{6,25},{7,24},{8,23},{9,... | collective-permute-start | bytes 786440 | tf_op jit(solution)/shard_map/ppermute | solution.py:952
  64.6 33.4 %collective-permute-start.1 = (f32[16,8,512]{2,1,0:T(8,128)S(1)}, f32[16,8,512]{2,1,0:T(8,128)S(1)}, u32[]{:S(2)}, u32[]{:S(2)}) collective-permute-start(f32[16,8,512]{2,1,0:T(8,128)S(1)} %copy-done.7), channel_id=1, source_target_pairs={{0,31},{1,30},{2,29},{3,28},{4,27},{5,26},{6,25},{7,24},{8,23},{9,... | collective-permute-start | bytes 786440 | tf_op jit(solution)/shard_map/ppermute | solution.py:953
  98.0 0.6 copy-start.5
  98.0 0.7 copy-start.2
  98.1 0.8 copy-start.3
  146.5 6.0 %copy-start.1 = (f32[32,8,1024]{2,1,0:T(8,128)}, f32[32,8,1024]{2,1,0:T(8,128)S(1)}, u32[]{:S(2)}) copy-start(f32[32,8,1024]{2,1,0:T(8,128)S(1)} %all_to_all.30.refs_0_) | copy-start | bytes 3145732
  152.5 29.8 %all-to-all-start.4 = ((f32[32,8,1024]{2,1,0:T(8,128)}), f32[32,8,1024]{2,1,0:T(8,128)S(1)}, u32[]{:S(2)}, u32[]{:S(2)}) async-start(f32[32,8,1024]{2,1,0:T(8,128)} %get-tuple-element.32), calls=%async_computation.4 | async-start | bytes 2097152 | tf_op jit(solution)/shard_map/all_to_all | solution.py:896
  182.3 4.6 %copy-start = (f32[32,8,1024]{2,1,0:T(8,128)}, f32[32,8,1024]{2,1,0:T(8,128)S(1)}, u32[]{:S(2)}) copy-start(f32[32,8,1024]{2,1,0:T(8,128)S(1)} %all-to-all-done.4.refs_0_.refs_1_) | copy-start | bytes 3145732
  187.0 21.6 %all-to-all-start.5 = ((f32[32,8,640]{2,1,0:T(8,128)}), f32[32,8,640]{2,1,0:T(8,128)S(1)}, u32[]{:S(2)}, u32[]{:S(2)}) async-start(f32[32,8,640]{2,1,0:T(8,128)} %shard_map.175), calls=%async_computation.5 | async-start | bytes 1310720 | tf_op jit(solution)/shard_map/all_to_all | solution.py:896
